TPU v7x, 32 devices: a whole 2x2x4 slice. The times are simulated.
32 devices in a mesh: member: 4 (over y, core), dp: 4 (over z), tensor: 2 (over x).
Axes of the slice: x: 2, y: 2, z: 4, core: 2. Of those that a mesh axis runs over, the one named last changes fastest.
Arguments:
- context: bfloat16 [2048, 5120], P(('member', 'dp'), 'tensor'), parts along dimension 0, may hold values from -6 to 6
- out_weight: bfloat16 [20480, 5120], P(('member', 'tensor'), 'dp'), parts along dimension 0, may hold values from -0.078125 to 0.078125
- residual: bfloat16 [2048, 5120], P(('member', 'dp', 'tensor')), parts along dimension 0, may hold values from -16 to 16
- norm_gain: float32 [20480], P('member'), parts along dimension 0, may hold values from 0.5 to 1.5
- head_weight: bfloat16 [38016, 5120], P(('member', 'dp', 'tensor')), parts along dimension 0, may hold values from -8 to 8
- targets: int32 [2048], P('member'), parts along dimension 0, may hold values from 0 to 9503
Outputs:
- stream: bfloat16 [2048, 5120], P(('member', 'dp', 'tensor')), parts along dimension 0
- token_loss: float32 [2048], P(('member', 'dp', 'tensor')), parts along dimension 0
There are 4 independent parts, one for each index of `member`. A program takes and returns all parts, laid end to end along the dimension named above; each array names one. Nothing has to cross between parts.
All inputs are finite; a program needn't handle non-finite values.
Results may differ from a plain program's by a relative error of at most 0.001.
Values may be sent and summed in bfloat16 or wider, within the bound.
No kernel may reach another device: no remote copies, remote signals or barrier semaphores. Data moves between devices by JAX's collectives and lax.ppermute only.
A program may use at most 128 MiB of HBM per device.

v0:
```python
import jax
import jax.numpy as jnp
from jax import lax
from jax.sharding import PartitionSpec as P

EPSILON = 1e-06


def merged(value, axis, join):
    pieces = jax.tree.map(lambda part: lax.all_gather(part, axis), value)
    head = jax.tree.map(lambda part: part[0], pieces)
    tail = jax.tree.map(lambda part: part[1:], pieces)
    subtotal, _ = lax.scan(lambda subtotal, share: (join(subtotal, share), None), head, tail)
    return subtotal


def normalize(stream, norm_gain):
    values = stream.astype(jnp.float32)
    mean_square = jnp.mean(values * values, axis=-1, keepdims=True)
    return (values * lax.rsqrt(mean_square + EPSILON) * norm_gain).astype(jnp.bfloat16)


def row_stats(normed_rows, head_weight, targets, vocab_start):
    logits = lax.dot_general(
        normed_rows, head_weight, (((1,), (1,)), ((), ())), preferred_element_type=jnp.float32
    )
    highest = jnp.max(logits, axis=1)
    summed = jnp.sum(jnp.exp(logits - highest[:, None]), axis=1)
    wanted = targets - vocab_start
    columns = jnp.arange(head_weight.shape[0], dtype=jnp.int32)[None, :]
    picked = jnp.sum(jnp.where(columns == wanted[:, None], logits, 0.0), axis=1)
    return (highest, summed, picked)


def combine(first, second):
    first_max, first_sum, first_pick = first
    second_max, second_sum, second_pick = second
    joined_max = jnp.maximum(first_max, second_max)
    joined_sum = first_sum * jnp.exp(first_max - joined_max) + second_sum * jnp.exp(
        second_max - joined_max
    )
    return (joined_max, joined_sum, first_pick + second_pick)


def local(context, out_weight, residual, norm_gain, head_weight, targets):
    vocab_start = lax.axis_index(("dp", "tensor")) * head_weight.shape[0]
    local_rows = residual.shape[0]
    dp_count = lax.axis_size("dp")
    tensor_count = lax.axis_size("tensor")
    shared = None
    head_terms = jnp.dot(
        lax.all_gather(context, "dp", axis=0, tiled=True),
        out_weight,
        preferred_element_type=jnp.float32,
    )
    column_width = head_terms.shape[1]
    ordered = head_terms.reshape(dp_count, tensor_count, local_rows, column_width)
    ordered = jnp.transpose(ordered, (1, 0, 2, 3)).reshape(
        tensor_count * dp_count * local_rows, column_width
    )
    my_columns = lax.psum_scatter(ordered, "tensor", scatter_dimension=0, tiled=True)
    shared = lax.all_to_all(my_columns, "dp", split_axis=0, concat_axis=1, tiled=True)
    stream = (residual.astype(jnp.float32) + shared).astype(jnp.bfloat16)
    normed = normalize(stream, norm_gain)
    fresh = row_stats(
        lax.all_gather(normed, ("dp", "tensor"), axis=0, tiled=True),
        head_weight,
        targets,
        vocab_start,
    )
    gathered = tuple((update for update in fresh))
    row_max, row_sum, row_pick = merged(gathered, ("dp", "tensor"), combine)
    losses = jnp.log(row_sum) + row_max - row_pick
    first_row = lax.axis_index(("dp", "tensor")) * local_rows
    token_loss = lax.dynamic_slice_in_dim(losses, first_row, local_rows, 0)
    return (stream, token_loss)


def solution(mesh):
    return jax.shard_map(
        local,
        mesh=mesh,
        in_specs=(
            P(("member", "dp"), "tensor"),
            P(("member", "tensor"), "dp"),
            P(("member", "dp", "tensor"), None),
            P("member"),
            P(("member", "dp", "tensor"), None),
            P("member"),
        ),
        out_specs=(P(("member", "dp", "tensor"), None), P(("member", "dp", "tensor"))),
        check_vma=False,
    )
```

profile of v0, /device:TPU:0, one launch (start us, length us, event | category | flops | bytes accessed | tf_op | source)
XLA Modules:
  0.0 332.1 jit_solution(5788330741261144011)
XLA Ops:
  7.2 0.0 all-gather.9.cloned.1.call-start
  7.2 0.7 all-gather.9.cloned.1.call-update
  7.9 0.0 reduce-scatter.2.cloned.1.call-start
  7.9 59.1 %all-gather.9.cloned.1.call-done = bf16[512,2560]{1,0:T(8,128)(2,1)} async-done(((bf16[128,2560]{1,0:T(8,128)(2,1)}), bf16[512,2560]{1,0:T(8,128)(2,1)}) %all-gather.9.cloned.1.call-update) | async-done | bytes 2621456 | tf_op jit(solution)/shard_map/all_gather | solution.py:52
  67.0 7.2 %fusion.4 = f32[512,1280]{1,0:T(8,128)S(1)} fusion(bf16[512,2560]{1,0:T(8,128)(2,1)} %all-gather.9.cloned.1.call-done, bf16[2560,1280]{1,0:T(8,128)(2,1)} %param.9), kind=kOutput, calls=%fused_computation.20 | convolution fusion | flops 3355443200 | bytes 11796480 | tf_op jit(solution)/shard_map/dot_general | solution.py:51
  74.2 1.7 copy.11
  75.9 0.0 reduce-scatter.2.cloned.1.call-update
  76.0 0.0 all-gather.11.cloned.1.call-start
  76.0 36.5 %reduce-scatter.2.cloned.1.call-done = f32[256,1280]{1,0:T(8,128)} async-done(((f32[512,1280]{1,0:T(8,128)}), f32[256,1280]{1,0:T(8,128)}) %reduce-scatter.2.cloned.1.call-update) | async-done | bytes 1310736 | tf_op jit(solution)/shard_map/reduce_scatter | solution.py:61
  112.6 0.0 copy-start.1
  112.6 35.9 %all_to_all.19 = f32[4,64,1280]{2,1,0:T(8,128)S(1)} all-to-all(f32[4,64,1280]{2,1,0:T(8,128)} %bitcast.40), channel_id=1, replica_groups=mesh['member'=4,'dp'=4,'tensor'=2] {'dp'}, dimensions={0} | all-to-all | bytes 2621440 | tf_op jit(solution)/shard_map/all_to_all | solution.py:62
  148.5 0.0 copy-start.2
  148.5 0.1 copy.16
  148.6 0.0 copy-start.3
  148.6 0.0 copy-done.1
  148.6 0.3 fusion
  148.9 0.0 copy-start
  148.9 0.3 copy-done.2
  149.2 1.1 fusion.2
  150.3 0.0 all-gather.11.cloned.1.call-update
  150.3 0.0 copy-done.3
  150.4 84.1 %all-gather.11.cloned.1.call-done = bf16[512,5120]{1,0:T(8,128)(2,1)} async-done(((bf16[64,5120]{1,0:T(8,128)(2,1)}), bf16[512,5120]{1,0:T(8,128)(2,1)}) %all-gather.11.cloned.1.call-update) | async-done | bytes 5242896 | tf_op jit(solution)/shard_map/all_gather | solution.py:66
  234.5 10.8 %fusion.3 = (f32[512]{0:T(512)S(1)}, f32[512,1188]{0,1:T(8,128)S(1)}) fusion(bf16[512,5120]{1,0:T(8,128)(2,1)} %all-gather.11.cloned.1.call-done, bf16[1188,5120]{1,0:T(8,128)(2,1)} %param.12), kind=kOutput, calls=%fused_computation.19 | convolution fusion | flops 6229149184 | bytes 19843072 | tf_op jit(solution)/shard_map/dot_general | solution.py:24
  245.3 0.0 copy-done
  245.3 0.7 select_reduce_fusion
  246.0 26.1 %all-gather.4 = f32[8,1,512]{2,1,0:T(1,128)S(1)} all-gather(f32[1,1,512]{2,1,0:T(1,128)S(1)} %bitcast.52), channel_id=3, replica_groups=mesh['member'=4,'dp'=4,'tensor'=2] {'dp','tensor'}, dimensions={0}, use_global_device_ids=true | all-gather | bytes 18432 | tf_op jit(solution)/shard_map/all_gather | solution.py:10
  272.1 26.1 %all-gather.5 = f32[8,1,512]{2,1,0:T(1,128)S(1)} all-gather(f32[1,1,512]{2,1,0:T(1,128)S(1)} %bitcast.51), channel_id=4, replica_groups=mesh['member'=4,'dp'=4,'tensor'=2] {'dp','tensor'}, dimensions={0}, use_global_device_ids=true | all-gather | bytes 18432 | tf_op jit(solution)/shard_map/all_gather | solution.py:10
  298.2 26.1 %all-gather.3 = f32[8,1,512]{2,1,0:T(1,128)S(1)} all-gather(f32[1,1,512]{2,1,0:T(1,128)S(1)} %bitcast.50), channel_id=2, replica_groups=mesh['member'=4,'dp'=4,'tensor'=2] {'dp','tensor'}, dimensions={0}, use_global_device_ids=true | all-gather | bytes 18432 | tf_op jit(solution)/shard_map/all_gather | solution.py:10
  324.3 0.6 while.14
  324.9 0.6 dynamic_slice.13
  (40 shorter events, 0.4 us)
Async XLA Ops:
  7.2 59.9 %all-gather.9.cloned.1.call-start = ((), (), s32[]{:S(2)}) async-start(), calls=%async_computation.2 | async-start | bytes 3276800 | tf_op jit(solution)/shard_map/all_gather | solution.py:52
  7.9 104.7 %reduce-scatter.2.cloned.1.call-start = ((), (), s32[]{:S(2)}) async-start(), calls=%async_computation.3 | async-start | bytes 3932160 | tf_op jit(solution)/shard_map/reduce_scatter | solution.py:61
  76.0 158.5 %all-gather.11.cloned.1.call-start = ((), (), s32[]{:S(2)}) async-start(), calls=%async_computation.4 | async-start | bytes 5898240 | tf_op jit(solution)/shard_map/all_gather | solution.py:66
  112.6 36.0 %copy-start.1 = (bf16[64,5120]{1,0:T(8,128)(2,1)S(1)}, bf16[64,5120]{1,0:T(8,128)(2,1)}, u32[]{:S(2)}) copy-start(bf16[64,5120]{1,0:T(8,128)(2,1)} %param.10) | copy-start | bytes 1966084
  148.5 0.7 copy-start.2
  148.6 1.7 copy-start.3
  148.9 96.4 %copy-start = (bf16[64,5120]{1,0:T(8,128)(2,1)}, bf16[64,5120]{1,0:T(8,128)(2,1)S(1)}, u32[]{:S(2)}) copy-start(bf16[64,5120]{1,0:T(8,128)(2,1)S(1)} %get-tuple-element.63) | copy-start | bytes 1966084
Sparse Core Ops, SparseCore 0:
  9.5 57.4 all-gather.8
  76.1 36.4 reduce-scatter.1
  150.4 83.9 all-gather.10
where the time goes:
time: 332 us
  waiting for transfers between devices  180 us (54%)
  blocking collectives  114 us (34%)
  matrix products  18 us (5%)
  between operations  13.9 us (4%)
    all_gather x1, waiting for transfers between devices, local(): lax.all_gather(normed, ('dp', 'tensor'), axis=0, tiled=True)  84.1 us
    all_gather x3, blocking collectives, merged(): pieces = jax.tree.map(lambda part: lax.all_gather(part, axis), value)  78.3 us
    all_gather x1, waiting for transfers between devices, local(): lax.all_gather(context, 'dp', axis=0, tiled=True)  59.1 us
    reduce_scatter x1, waiting for transfers between devices, local(): lax.psum_scatter(ordered, 'tensor', scatter_dimension=0, tiled=True)  36.5 us
    all_to_all x1, blocking collectives, local(): lax.all_to_all(my_columns, 'dp', split_axis=0, concat_axis=1, tiled=True)  35.9 us
    dot_general x1, matrix products, row_stats(): lax.dot_general(normed_rows, head_weight, (((1,), (1,)), ((), ())), prefe...  10.8 us
    dot_general x1, matrix products, local(): jnp.dot(lax.all_gather(context, 'dp', axis=0, tiled=True), out_weight, pr...  7.2 us
  transfers between devices with their start and end apart: 3, of which 3 were waited for; matrix products, arithmetic and copies ran while one was open for 0% of the time, Pallas kernels for 0%

commit v1 on v0

v1 whole, which is shorter than its diff:
```python
import functools

import jax
import jax.numpy as jnp
from jax import lax
from jax.experimental import pallas as pl
from jax.experimental.pallas import tpu as pltpu
from jax.sharding import PartitionSpec as P


EPSILON = 1e-06


def halves(local_rows):
    return 2 if local_rows % 64 == 0 else 1


def ahead(value, shift, count):
    moved = value + shift
    return jnp.where(moved >= count, moved - count, moved)


def behind(value, shift, count):
    moved = value - shift
    return jnp.where(moved < 0, moved + count, moved)


def head_kernel(shape, where_ref, wanted_ref, gain_ref, weight_ref, *rest):
    dp_count, tensor_count, rows, columns, vocab = shape
    blocks = rest[: dp_count * tensor_count]
    out_ref, normed_ref = rest[dp_count * tensor_count :]
    step = pl.program_id(0)

    @pl.when(step == 0)
    def _():
        start = where_ref[0]
        for j in range(tensor_count):
            for rho in range(dp_count):
                taken = []
                squares = jnp.zeros((rows, 1), jnp.float32)
                for k in range(dp_count):
                    s = (rho - k) % dp_count
                    value = blocks[j * dp_count + k][s * rows : (s + 1) * rows, :]
                    value = value.astype(jnp.float32)
                    squares = squares + jnp.sum(value * value, axis=1, keepdims=True)
                    taken.append(value)
                scale = lax.rsqrt(squares / (dp_count * columns) + EPSILON)
                first = (j * dp_count + rho) * rows
                for k, value in enumerate(taken):
                    owner = start - k
                    owner = jnp.where(owner < 0, owner + dp_count, owner)
                    at = pl.multiple_of(owner * columns, columns)
                    gain = gain_ref[:, pl.ds(at, columns)]
                    normed_ref[first : first + rows, pl.ds(at, columns)] = (
                        value * scale * gain
                    ).astype(jnp.bfloat16)
        count = out_ref.shape[1]
        out_ref[0:1, :] = jnp.full((1, count), -jnp.inf, jnp.float32)
        out_ref[1:3, :] = jnp.zeros((2, count), jnp.float32)

    logits = lax.dot_general(
        weight_ref[...],
        normed_ref[...],
        (((1,), (1,)), ((), ())),
        preferred_element_type=jnp.float32,
    )
    entry = lax.broadcasted_iota(jnp.int32, logits.shape, 0) + step * logits.shape[0]
    masked = jnp.where(entry < vocab, logits, -jnp.inf)
    before = out_ref[0:1, :]
    highest = jnp.maximum(before, jnp.max(masked, axis=0, keepdims=True))
    out_ref[1:2, :] = out_ref[1:2, :] * jnp.exp(before - highest) + jnp.sum(
        jnp.exp(masked - highest), axis=0, keepdims=True
    )
    out_ref[0:1, :] = highest
    hit = jnp.logical_and(entry == wanted_ref[...], entry < vocab)
    out_ref[2:3, :] = out_ref[2:3, :] + jnp.sum(
        jnp.where(hit, logits, 0.0), axis=0, keepdims=True
    )


def head_stats(blocks, d, wanted, norm_gain, head_weight, shape):
    dp_count, tensor_count, rows, columns, vocab = shape
    count = dp_count * tensor_count * rows
    width = dp_count * columns
    steps = 5
    entries = -(-vocab // (steps * 16)) * 16
    steps = -(-vocab // entries)
    return pl.pallas_call(
        functools.partial(head_kernel, shape),
        grid=(steps,),
        in_specs=[
            pl.BlockSpec(memory_space=pltpu.SMEM),
            pl.BlockSpec((1, count), lambda i: (0, 0)),
            pl.BlockSpec((1, width), lambda i: (0, 0)),
            pl.BlockSpec((entries, width), lambda i: (i, 0)),
        ]
        + [pl.BlockSpec(memory_space=pltpu.VMEM)] * len(blocks),
        out_specs=pl.BlockSpec((3, count), lambda i: (0, 0)),
        out_shape=jax.ShapeDtypeStruct((3, count), jnp.float32),
        scratch_shapes=[pltpu.VMEM((count, width), jnp.bfloat16)],
        compiler_params=pltpu.CompilerParams(
            dimension_semantics=("arbitrary",), vmem_limit_bytes=40 * 1024 * 1024
        ),
        cost_estimate=pl.CostEstimate(
            flops=2 * count * width * vocab,
            bytes_accessed=2 * vocab * width + 4 * count * width,
            transcendentals=count * vocab,
        ),
        name="head_stats",
    )(d.reshape(1), wanted, norm_gain, head_weight, *blocks)


def local(context, out_weight, residual, norm_gain, head_weight, targets):
    dp_count = lax.axis_size("dp")
    tensor_count = lax.axis_size("tensor")
    d = lax.axis_index("dp")
    t = lax.axis_index("tensor")
    local_rows, width = residual.shape
    parts = halves(local_rows)
    rows = local_rows // parts
    depth = context.shape[1]
    columns = out_weight.shape[1]
    vocab = head_weight.shape[0]
    vocab_start = (d * tensor_count + t) * vocab

    def along_dp(value, shift):
        return lax.ppermute(
            value, "dp", [(i, (i + shift) % dp_count) for i in range(dp_count)]
        )

    def along_tensor(value, shift):
        return lax.ppermute(
            value, "tensor", [(i, (i + shift) % tensor_count) for i in range(tensor_count)]
        )

    residuals = []
    for s in range(dp_count):
        cut = lax.dynamic_slice(
            residual, (0, ahead(d, s, dp_count) * columns), (local_rows, columns)
        )
        residuals.append(along_dp(cut, s) if s else cut)

    by_tensor = context.reshape(tensor_count, parts, rows, depth)
    gathered = []
    for h in range(parts):
        held = jnp.concatenate(
            [
                lax.dynamic_index_in_dim(
                    by_tensor[:, h], ahead(t, 1 + j, tensor_count) if j + 1 < tensor_count else t, 0, keepdims=False
                )
                for j in range(tensor_count)
            ],
            axis=0,
        )
        pieces = []
        for s in range(dp_count):
            if s:
                held = along_dp(held, 1)
            partial = jnp.dot(held, out_weight, preferred_element_type=jnp.float32)
            total = partial[(tensor_count - 1) * rows :]
            for j in range(1, tensor_count):
                total = total + along_tensor(partial[(j - 1) * rows : j * rows], j)
            mine = residuals[s][h * rows : (h + 1) * rows]
            if h:
                mine, _ = lax.optimization_barrier((mine, gathered[h - 1][0][0]))
            mine = mine.astype(jnp.float32)
            pieces.append((mine + total).astype(jnp.bfloat16))
        block = jnp.concatenate(pieces, axis=0)
        arrived = []
        for k in range(dp_count):
            if k:
                block = along_dp(block, 1)
            arrived.append([block] + [along_tensor(block, j) for j in range(1, tensor_count)])
        gathered.append(arrived)

    def spread(parts_by_k):
        rows_out = parts_by_k[0].shape[0]
        out = jnp.zeros((rows_out, width), jnp.bfloat16)
        for k, value in enumerate(parts_by_k):
            column = behind(d, k, dp_count) * columns
            out = lax.dynamic_update_slice(out, value, (0, column))
        return out

    def block_rows(block, rho, k):
        s = (rho - k) % dp_count
        return block[s * rows : (s + 1) * rows]

    stream = spread(
        [
            jnp.concatenate([block_rows(gathered[h][k][0], 0, k) for h in range(parts)], axis=0)
            for k in range(dp_count)
        ]
    )

    target_table = targets.reshape(dp_count, tensor_count, parts, rows) - vocab_start
    stats = []
    for h in range(parts):
        wanted = jnp.concatenate(
            [
                target_table[behind(d, rho, dp_count), behind(t, j, tensor_count), h]
                for j in range(tensor_count)
                for rho in range(dp_count)
            ]
        )
        blocks = [gathered[h][k][j] for j in range(tensor_count) for k in range(dp_count)]
        stats.append(
            head_stats(
                blocks,
                d,
                wanted[None, :],
                norm_gain[None, :],
                head_weight,
                (dp_count, tensor_count, rows, columns, vocab),
            )
        )

    table = jnp.stack(stats).reshape(parts, 3, tensor_count, dp_count, rows)
    table = jnp.transpose(table, (3, 2, 1, 0, 4)).reshape(
        dp_count, tensor_count, 3, local_rows
    )
    table = jnp.take(table, behind(d, jnp.arange(dp_count), dp_count), axis=0)
    table = jnp.take(
        table, behind(t, jnp.arange(tensor_count), tensor_count), axis=1
    )
    table = table.reshape(dp_count * tensor_count, 3, local_rows)
    table = lax.all_to_all(table, ("dp", "tensor"), 0, 0, tiled=True)
    row_max = jnp.max(table[:, 0], axis=0)
    row_sum = jnp.sum(table[:, 1] * jnp.exp(table[:, 0] - row_max[None]), axis=0)
    token_loss = jnp.log(row_sum) + row_max - jnp.sum(table[:, 2], axis=0)
    return (stream, token_loss)


def solution(mesh):
    def program(context, out_weight, residual, norm_gain, head_weight, targets):
        step = jax.shard_map(
            local,
            mesh=mesh,
            in_specs=(
                P(("member", "dp"), "tensor"),
                P(("member", "tensor"), "dp"),
                P(("member", "dp", "tensor"), None),
                P("member"),
                P(("member", "dp", "tensor"), None),
                P("member"),
            ),
            out_specs=(P(("member", "dp", "tensor"), None), P(("member", "dp", "tensor"))),
            check_vma=False,
        )
        return step(context, out_weight, residual, norm_gain, head_weight, targets)

    return program
```

time: 332 us -> 192 us (0.58)
  blocking collectives: 114 us -> 0 us
  waiting for transfers between devices: 180 us -> 90.7 us
  starting transfers between devices: 0.12 us -> 44 us
  Pallas kernels: 0 us -> 18.2 us
  between operations: 13.9 us -> 1.09 us
  local copies, waits for them, and re-layouts: 2.84 us -> 10 us
  other arithmetic: 2.29 us -> 9.12 us
    all_gather x2 -> x0, waiting for transfers between devices: 143 us -> none  [the longest x1 84.1 us: local(): lax.all_gather(normed, ('dp', 'tensor'), axis=0, tiled=True)]
    ppermute x0 -> x31, waiting for transfers between devices: none -> 84.9 us  [the longest x15 60.5 us: along_dp(): lax.ppermute(value, 'dp', [(i, (i + shift) % dp_count) for i in range(dp_...]
    all_gather x3 -> x0, blocking collectives: 78.3 us -> none  [merged(): pieces = jax.tree.map(lambda part: lax.all_gather(part, axis), value)]
    ppermute x0 -> x31, starting transfers between devices: none -> 38.3 us  [the longest x15 19.3 us: along_dp(): lax.ppermute(value, 'dp', [(i, (i + shift) % dp_count) for i in range(dp_...]
    reduce_scatter x1 -> x0, waiting for transfers between devices: 36.5 us -> none  [local(): lax.psum_scatter(ordered, 'tensor', scatter_dimension=0, tiled=True)]
    all_to_all x1 -> x0, blocking collectives: 35.9 us -> none  [local(): lax.all_to_all(my_columns, 'dp', split_axis=0, concat_axis=1, tiled=True)]
    pallas_call x0 -> x2, Pallas kernels: none -> 18.2 us  [head_stats(): pl.pallas_call(functools.partial(head_kernel, shape), grid=(steps,), in_s...]
    all_to_all x0 -> x1, waiting for transfers between devices: none -> 5.83 us  [local(): table = lax.all_to_all(table, ('dp', 'tensor'), 0, 0, tiled=True)]
  transfers between devices with their start and end apart: 3 -> 32, of which waited for: 3 -> 18; matrix products, arithmetic and copies ran while one was open for 0% -> 14% of each run, Pallas kernels for 0% -> 5%
where the time goes in v1:
time: 192 us
  waiting for transfers between devices  90.7 us (47%)
  starting transfers between devices  44 us (23%)
  matrix products  18.8 us (10%)
  Pallas kernels  18.2 us (9%)
  local copies, waits for them, and re-layouts  10 us (5%)
  other arithmetic  9.12 us (5%)
    ppermute x15, waiting for transfers between devices, along_dp(): lax.ppermute(value, 'dp', [(i, (i + shift) % dp_count) for i in range(dp_...  60.5 us
    ppermute x16, waiting for transfers between devices, along_tensor(): lax.ppermute(value, 'tensor', [(i, (i + shift) % tensor_count) for i in r...  24.4 us
    ppermute x15, starting transfers between devices, along_dp(): lax.ppermute(value, 'dp', [(i, (i + shift) % dp_count) for i in range(dp_...  19.3 us
    ppermute x16, starting transfers between devices, along_tensor(): lax.ppermute(value, 'tensor', [(i, (i + shift) % tensor_count) for i in r...  18.9 us
    dot_general x8, matrix products, local(): partial = jnp.dot(held, out_weight, preferred_element_type=jnp.float32)  18.8 us
    pallas_call x2, Pallas kernels, head_stats(): pl.pallas_call(functools.partial(head_kernel, shape), grid=(steps,), in_s...  18.2 us
    all_to_all x1, waiting for transfers between devices, local(): table = lax.all_to_all(table, ('dp', 'tensor'), 0, 0, tiled=True)  5.83 us
    all_to_all x1, starting transfers between devices, local(): table = lax.all_to_all(table, ('dp', 'tensor'), 0, 0, tiled=True)  5.73 us
  transfers between devices with their start and end apart: 32, of which 18 were waited for; matrix products, arithmetic and copies ran while one was open for 14% of the time, Pallas kernels for 5%

profile of v1, /device:TPU:0, one launch (start us, length us, event | category | flops | bytes accessed | tf_op | source)
XLA Modules:
  0.0 191.9 jit_solution(5988764143160885781)
XLA Ops:
  1.9 4.1 %fusion.35 = f32[64,1280]{1,0:T(8,128)S(1)} fusion(bf16[2560,1280]{1,0:T(8,128)(2,1)} %param.7, bf16[32,2560]{1,0:T(8,128)(2,1)S(1)} %get-tuple-element.39, bf16[32,2560]{1,0:T(8,128)(2,1)S(1)} %get-tuple-element.40), kind=kOutput, calls=%fused_computation.96 | convolution fusion | flops 420085760 | bytes 7208960 | tf_op jit(solution)/shard_map/dot_general | solution.py:159
  6.7 3.0 %collective-permute-start = (f32[32,1280]{1,0:T(8,128)}, f32[32,1280]{1,0:T(8,128)}, u32[]{:S(2)}, u32[]{:S(2)}) collective-permute-start(f32[32,1280]{1,0:T(8,128)} %slice.149), channel_id=1, source_target_pairs={{0,1},{1,0},{2,3},{3,2},{4,5},{5,4},{6,7},{7,6},{8,9},{9,8},{10,11... | collective-permute-start | bytes 491528 | tf_op jit(solution)/shard_map/ppermute | solution.py:132
  10.5 1.6 collective-permute-start.1
  12.8 1.6 collective-permute-start.2
  15.6 2.7 %collective-permute-start.7 = (bf16[64,1280]{1,0:T(8,128)(2,1)}, bf16[64,1280]{1,0:T(8,128)(2,1)S(1)}, u32[]{:S(2)}, u32[]{:S(2)}) collective-permute-start(bf16[64,1280]{1,0:T(8,128)(2,1)} %get-tuple-element.13), channel_id=1, source_target_pairs={{0,6},{2,0},{4,2},{6,4},{1,7},{3,1},{5,3},{7,5},{8,14},{10,8},{12,... | collective-permute-start | bytes 491528 | tf_op jit(solution)/shard_map/ppermute | solution.py:127
  19.1 4.3 %fusion.34 = f32[64,1280]{1,0:T(8,128)S(1)} fusion(bf16[2560,1280]{1,0:T(8,128)(2,1)} %param.7, bf16[32,2560]{1,0:T(8,128)(2,1)S(1)} %get-tuple-element.20, bf16[32,2560]{1,0:T(8,128)(2,1)S(1)} %get-tuple-element.19), kind=kOutput, calls=%fused_computation.95 | convolution fusion | flops 420085760 | bytes 7208960 | tf_op jit(solution)/shard_map/dot_general | solution.py:159
  25.2 8.6 %collective-permute-done.4 = bf16[64,1280]{1,0:T(8,128)(2,1)} collective-permute-done((bf16[64,1280]{1,0:T(8,128)(2,1)}, bf16[64,1280]{1,0:T(8,128)(2,1)}, u32[]{:S(2)}, u32[]{:S(2)}) %collective-permute-start.4) | collective-permute-done | bytes 163872 | tf_op jit(solution)/shard_map/ppermute | solution.py:127
  37.1 4.2 %fusion.37 = f32[64,1280]{1,0:T(8,128)S(1)} fusion(bf16[64,2560]{1,0:T(8,128)(2,1)} %collective-permute-done.2, bf16[2560,1280]{1,0:T(8,128)(2,1)} %param.7), kind=kOutput, calls=%fused_computation.98 | convolution fusion | flops 419430400 | bytes 7208960 | tf_op jit(solution)/shard_map/dot_general | solution.py:159
  41.4 1.8 collective-permute-start.3
  44.9 7.9 %collective-permute-start.5 = (bf16[64,2560]{1,0:T(8,128)(2,1)}, bf16[64,2560]{1,0:T(8,128)(2,1)S(1)}, u32[]{:S(2)}, u32[]{:S(2)}) collective-permute-start(bf16[64,2560]{1,0:T(8,128)(2,1)} %collective-permute-done.2), channel_id=1, source_target_pairs={{0,2},{2,4},{4,6},{6,0},{1,3},{3,5},{5,7},{7,1},{8,10},{10,12},{12... | collective-permute-start | bytes 983048 | tf_op jit(solution)/shard_map/ppermute | solution.py:127
  53.7 7.5 %collective-permute-done.5 = bf16[64,2560]{1,0:T(8,128)(2,1)S(1)} collective-permute-done((bf16[64,2560]{1,0:T(8,128)(2,1)}, bf16[64,2560]{1,0:T(8,128)(2,1)S(1)}, u32[]{:S(2)}, u32[]{:S(2)}) %collective-permute-start.5) | collective-permute-done | bytes 327712 | tf_op jit(solution)/shard_map/ppermute | solution.py:127
  63.1 3.5 %collective-permute-done.14 = bf16[64,2560]{1,0:T(8,128)(2,1)S(1)} collective-permute-done((bf16[64,2560]{1,0:T(8,128)(2,1)S(1)}, bf16[64,2560]{1,0:T(8,128)(2,1)S(1)}, u32[]{:S(2)}, u32[]{:S(2)}) %collective-permute-start.14) | collective-permute-done | bytes 327712 | tf_op jit(solution)/shard_map/ppermute | solution.py:127
  68.5 2.5 %collective-permute-start.8 = (bf16[64,2560]{1,0:T(8,128)(2,1)S(1)}, bf16[64,2560]{1,0:T(8,128)(2,1)S(1)}, u32[]{:S(2)}, u32[]{:S(2)}) collective-permute-start(bf16[64,2560]{1,0:T(8,128)(2,1)S(1)} %collective-permute-done.5), channel_id=1, source_target_pairs={{0,2},{2,4},{4,6},{6,0},{1,3},{3,5},{5,7},{7,1},{8,10},{10,12},{12... | collective-permute-start | bytes 983048 | tf_op jit(solution)/shard_map/ppermute | solution.py:127
  72.2 8.7 %collective-permute-done.8 = bf16[64,2560]{1,0:T(8,128)(2,1)S(1)} collective-permute-done((bf16[64,2560]{1,0:T(8,128)(2,1)S(1)}, bf16[64,2560]{1,0:T(8,128)(2,1)S(1)}, u32[]{:S(2)}, u32[]{:S(2)}) %collective-permute-start.8) | collective-permute-done | bytes 327712 | tf_op jit(solution)/shard_map/ppermute | solution.py:127
  82.2 1.6 collective-permute-start.9
  86.5 1.6 collective-permute-start.17
  89.3 2.6 %collective-permute-done.17 = f32[32,1280]{1,0:T(8,128)S(1)} collective-permute-done((f32[32,1280]{1,0:T(8,128)S(1)}, f32[32,1280]{1,0:T(8,128)S(1)}, u32[]{:S(2)}, u32[]{:S(2)}) %collective-permute-start.17) | collective-permute-done | bytes 163872 | tf_op jit(solution)/shard_map/ppermute | solution.py:132
  93.0 8.0 %collective-permute-done.11.rest_1_ = bf16[128,1280]{1,0:T(8,128)(2,1)S(1)} collective-permute-done((bf16[128,1280]{1,0:T(8,128)(2,1)S(1)}, bf16[128,1280]{1,0:T(8,128)(2,1)S(1)}, u32[]{:S(2)}, u32[]{:S(2)}) %collective-permute-start.11) | collective-permute-done | bytes 327712 | tf_op jit(solution)/shard_map/ppermute | solution.py:127
  101.0 7.0 %collective-permute-done.18.rest_1_ = bf16[128,1280]{1,0:T(8,128)(2,1)S(1)} collective-permute-done((bf16[128,1280]{1,0:T(8,128)(2,1)S(1)}, bf16[128,1280]{1,0:T(8,128)(2,1)S(1)}, u32[]{:S(2)}, u32[]{:S(2)}) %collective-permute-start.18) | collective-permute-done | bytes 327712 | tf_op jit(solution)/shard_map/ppermute | solution.py:127
  108.0 7.0 %collective-permute-done.19.rest_2_ = bf16[128,1280]{1,0:T(8,128)(2,1)S(1)} collective-permute-done((bf16[128,1280]{1,0:T(8,128)(2,1)S(1)}, bf16[128,1280]{1,0:T(8,128)(2,1)S(1)}, u32[]{:S(2)}, u32[]{:S(2)}) %collective-permute-start.19) | collective-permute-done | bytes 327712 | tf_op jit(solution)/shard_map/ppermute | solution.py:127
  115.0 1.6 collective-permute-start.23
  118.6 3.4 %collective-permute-done.20.rest_2_ = bf16[128,1280]{1,0:T(8,128)(2,1)S(1)} collective-permute-done((bf16[128,1280]{1,0:T(8,128)(2,1)S(1)}, bf16[128,1280]{1,0:T(8,128)(2,1)S(1)}, u32[]{:S(2)}, u32[]{:S(2)}) %collective-permute-start.20) | collective-permute-done | bytes 327712 | tf_op jit(solution)/shard_map/ppermute | solution.py:127
  123.6 5.2 %collective-permute-done.21.rest_3_ = bf16[128,1280]{1,0:T(8,128)(2,1)S(1)} collective-permute-done((bf16[128,1280]{1,0:T(8,128)(2,1)S(1)}, bf16[128,1280]{1,0:T(8,128)(2,1)S(1)}, u32[]{:S(2)}, u32[]{:S(2)}) %collective-permute-start.21) | collective-permute-done | bytes 327712 | tf_op jit(solution)/shard_map/ppermute | solution.py:127
  133.1 5.4 %collective-permute-done.25.rest_6_ = bf16[128,1280]{1,0:T(8,128)(2,1)S(1)} collective-permute-done((bf16[128,1280]{1,0:T(8,128)(2,1)S(1)}, bf16[128,1280]{1,0:T(8,128)(2,1)S(1)}, u32[]{:S(2)}, u32[]{:S(2)}) %collective-permute-start.25) | collective-permute-done | bytes 327712 | tf_op jit(solution)/shard_map/ppermute | solution.py:132
  141.2 4.3 %collective-permute-done.26.rest_7_ = bf16[128,1280]{1,0:T(8,128)(2,1)S(1)} collective-permute-done((bf16[128,1280]{1,0:T(8,128)(2,1)S(1)}, bf16[128,1280]{1,0:T(8,128)(2,1)S(1)}, u32[]{:S(2)}, u32[]{:S(2)}) %collective-permute-start.26) | collective-permute-done | bytes 327712 | tf_op jit(solution)/shard_map/ppermute | solution.py:132
  145.5 9.1 %head_stats.2 = f32[3,256]{1,0:T(4,128)S(1)} custom-call(s32[1]{0:T(128)} %bitcast.5.where_ref, s32[1,256]{1,0:T(1,128)S(1)} %bitcast.76, f32[1,5120]{1,0:T(1,128)S(1)} %bitcast.73, bf16[1188,5120]{1,0:T(8,128)(2,1)} %weight_ref.3, bf16[128,1280]{1,0:T(8,128)(2,1)S(1)} %pad_maximum_fusion.1.rest_0_, bf16[128,1280]{1,0:T(8,128)(2,1)S(1)} %collective-permute-done.11.rest_1_, ...), custom_call_target="tpu_custom_call" | custom-call | flops 3114270720 | bytes 17408000 | tf_op jit(solution)/shard_map/head_stats/pallas_call | solution.py:88
  154.7 4.8 %collective-permute-done.28.rest_5_ = bf16[128,1280]{1,0:T(8,128)(2,1)S(1)} collective-permute-done((bf16[128,1280]{1,0:T(8,128)(2,1)S(1)}, bf16[128,1280]{1,0:T(8,128)(2,1)S(1)}, u32[]{:S(2)}, u32[]{:S(2)}) %collective-permute-start.28) | collective-permute-done | bytes 327712 | tf_op jit(solution)/shard_map/ppermute | solution.py:132
  159.4 3.5 %collective-permute-done.29.rest_6_ = bf16[128,1280]{1,0:T(8,128)(2,1)S(1)} collective-permute-done((bf16[128,1280]{1,0:T(8,128)(2,1)S(1)}, bf16[128,1280]{1,0:T(8,128)(2,1)S(1)}, u32[]{:S(2)}, u32[]{:S(2)}) %collective-permute-start.29) | collective-permute-done | bytes 327712 | tf_op jit(solution)/shard_map/ppermute | solution.py:132
  163.0 3.5 %collective-permute-done.30.rest_7_ = bf16[128,1280]{1,0:T(8,128)(2,1)S(1)} collective-permute-done((bf16[128,1280]{1,0:T(8,128)(2,1)S(1)}, bf16[128,1280]{1,0:T(8,128)(2,1)S(1)}, u32[]{:S(2)}, u32[]{:S(2)}) %collective-permute-start.30) | collective-permute-done | bytes 327712 | tf_op jit(solution)/shard_map/ppermute | solution.py:132
  166.5 9.1 %head_stats.3 = f32[3,256]{1,0:T(4,128)S(1)} custom-call(s32[1]{0:T(128)} %bitcast.5.where_ref, s32[1,256]{1,0:T(1,128)S(1)} %bitcast.75, f32[1,5120]{1,0:T(1,128)S(1)} %bitcast.74, bf16[1188,5120]{1,0:T(8,128)(2,1)} %weight_ref.3, bf16[128,1280]{1,0:T(8,128)(2,1)S(1)} %pad_maximum_fusion.3.rest_0_, bf16[128,1280]{1,0:T(8,128)(2,1)S(1)} %collective-permute-done.18.rest_1_, ...), custom_call_target="tpu_custom_call" | custom-call | flops 3114270720 | bytes 17408000 | tf_op jit(solution)/shard_map/head_stats/pallas_call | solution.py:88
  177.8 5.7 %all-to-all-start = ((f32[8,1,192]{2,1,0:T(1,128)}), f32[8,1,192]{2,1,0:T(1,128)S(1)}, u32[]{:S(2)}, u32[]{:S(2)}) async-start(f32[8,1,192]{2,1,0:T(1,128)} %reshape.113), calls=%async_computation | async-start | bytes 16384 | tf_op jit(solution)/shard_map/all_to_all | solution.py:226
  184.2 5.8 %all-to-all-done = f32[8,1,192]{2,1,0:T(1,128)S(1)} async-done(((f32[8,1,192]{2,1,0:T(1,128)}), f32[8,1,192]{2,1,0:T(1,128)S(1)}, u32[]{:S(2)}, u32[]{:S(2)}) %all-to-all-start) | async-done | bytes 6176 | tf_op jit(solution)/shard_map/all_to_all | solution.py:226
  (135 shorter events, 39.9 us)
Async XLA Ops:
  6.7 29.0 %collective-permute-start = (f32[32,1280]{1,0:T(8,128)}, f32[32,1280]{1,0:T(8,128)}, u32[]{:S(2)}, u32[]{:S(2)}) collective-permute-start(f32[32,1280]{1,0:T(8,128)} %slice.149), channel_id=1, source_target_pairs={{0,1},{1,0},{2,3},{3,2},{4,5},{5,4},{6,7},{7,6},{8,9},{9,8},{10,11... | collective-permute-start | bytes 491528 | tf_op jit(solution)/shard_map/ppermute | solution.py:132
  10.5 13.8 %collective-permute-start.1 = (bf16[64,1280]{1,0:T(8,128)(2,1)}, bf16[64,1280]{1,0:T(8,128)(2,1)}, u32[]{:S(2)}, u32[]{:S(2)}) collective-permute-start(bf16[64,1280]{1,0:T(8,128)(2,1)} %get-tuple-element.12), channel_id=1, source_target_pairs={{0,2},{2,4},{4,6},{6,0},{1,3},{3,5},{5,7},{7,1},{8,10},{10,12},{12... | collective-permute-start | bytes 491528 | tf_op jit(solution)/shard_map/ppermute | solution.py:127
  12.8 24.3 %collective-permute-start.2 = (bf16[64,2560]{1,0:T(8,128)(2,1)}, bf16[64,2560]{1,0:T(8,128)(2,1)}, u32[]{:S(2)}, u32[]{:S(2)}) collective-permute-start(bf16[64,2560]{1,0:T(8,128)(2,1)} %pad_maximum_fusion), channel_id=1, source_target_pairs={{0,2},{2,4},{4,6},{6,0},{1,3},{3,5},{5,7},{7,1},{8,10},{10,12},{12... | collective-permute-start | bytes 983048 | tf_op jit(solution)/shard_map/ppermute | solution.py:127
  14.4 19.5 %collective-permute-start.4 = (bf16[64,1280]{1,0:T(8,128)(2,1)}, bf16[64,1280]{1,0:T(8,128)(2,1)}, u32[]{:S(2)}, u32[]{:S(2)}) collective-permute-start(bf16[64,1280]{1,0:T(8,128)(2,1)} %get-tuple-element.14), channel_id=1, source_target_pairs={{0,4},{2,6},{4,0},{6,2},{1,5},{3,7},{5,1},{7,3},{8,12},{10,14},{12... | collective-permute-start | bytes 491528 | tf_op jit(solution)/shard_map/ppermute | solution.py:127
  15.6 19.4 %collective-permute-start.7 = (bf16[64,1280]{1,0:T(8,128)(2,1)}, bf16[64,1280]{1,0:T(8,128)(2,1)S(1)}, u32[]{:S(2)}, u32[]{:S(2)}) collective-permute-start(bf16[64,1280]{1,0:T(8,128)(2,1)} %get-tuple-element.13), channel_id=1, source_target_pairs={{0,6},{2,0},{4,2},{6,4},{1,7},{3,1},{5,3},{7,5},{8,14},{10,8},{12,... | collective-permute-start | bytes 491528 | tf_op jit(solution)/shard_map/ppermute | solution.py:127
  24.3 18.9 %collective-permute-start.12 = (bf16[64,2560]{1,0:T(8,128)(2,1)}, bf16[64,2560]{1,0:T(8,128)(2,1)S(1)}, u32[]{:S(2)}, u32[]{:S(2)}) collective-permute-start(bf16[64,2560]{1,0:T(8,128)(2,1)} %pad_maximum_fusion.2), channel_id=1, source_target_pairs={{0,2},{2,4},{4,6},{6,0},{1,3},{3,5},{5,7},{7,1},{8,10},{10,12},{12... | collective-permute-start | bytes 983048 | tf_op jit(solution)/shard_map/ppermute | solution.py:127
  33.9 58.1 %collective-permute-start.10 = (f32[32,1280]{1,0:T(8,128)}, f32[32,1280]{1,0:T(8,128)S(1)}, u32[]{:S(2)}, u32[]{:S(2)}) collective-permute-start(f32[32,1280]{1,0:T(8,128)} %slice.161), channel_id=1, source_target_pairs={{0,1},{1,0},{2,3},{3,2},{4,5},{5,4},{6,7},{7,6},{8,9},{9,8},{10,11... | collective-permute-start | bytes 491528 | tf_op jit(solution)/shard_map/ppermute | solution.py:132
  41.4 11.4 %collective-permute-start.3 = (f32[32,1280]{1,0:T(8,128)S(1)}, f32[32,1280]{1,0:T(8,128)S(1)}, u32[]{:S(2)}, u32[]{:S(2)}) collective-permute-start(f32[32,1280]{1,0:T(8,128)S(1)} %slice.152), channel_id=1, source_target_pairs={{0,1},{1,0},{2,3},{3,2},{4,5},{5,4},{6,7},{7,6},{8,9},{9,8},{10,11... | collective-permute-start | bytes 491528 | tf_op jit(solution)/shard_map/ppermute | solution.py:132
  44.5 44.8 %collective-permute-start.13 = (f32[32,1280]{1,0:T(8,128)S(1)}, f32[32,1280]{1,0:T(8,128)S(1)}, u32[]{:S(2)}, u32[]{:S(2)}) collective-permute-start(f32[32,1280]{1,0:T(8,128)S(1)} %slice.165), channel_id=1, source_target_pairs={{0,1},{1,0},{2,3},{3,2},{4,5},{5,4},{6,7},{7,6},{8,9},{9,8},{10,11... | collective-permute-start | bytes 491528 | tf_op jit(solution)/shard_map/ppermute | solution.py:132
  44.9 16.3 %collective-permute-start.5 = (bf16[64,2560]{1,0:T(8,128)(2,1)}, bf16[64,2560]{1,0:T(8,128)(2,1)S(1)}, u32[]{:S(2)}, u32[]{:S(2)}) collective-permute-start(bf16[64,2560]{1,0:T(8,128)(2,1)} %collective-permute-done.2), channel_id=1, source_target_pairs={{0,2},{2,4},{4,6},{6,0},{1,3},{3,5},{5,7},{7,1},{8,10},{10,12},{12... | collective-permute-start | bytes 983048 | tf_op jit(solution)/shard_map/ppermute | solution.py:127
  52.8 13.8 %collective-permute-start.14 = (bf16[64,2560]{1,0:T(8,128)(2,1)S(1)}, bf16[64,2560]{1,0:T(8,128)(2,1)S(1)}, u32[]{:S(2)}, u32[]{:S(2)}) collective-permute-start(bf16[64,2560]{1,0:T(8,128)(2,1)S(1)} %collective-permute-done.12), channel_id=1, source_target_pairs={{0,2},{2,4},{4,6},{6,0},{1,3},{3,5},{5,7},{7,1},{8,10},{10,12},{12... | collective-permute-start | bytes 983048 | tf_op jit(solution)/shard_map/ppermute | solution.py:127
  62.5 8.5 %collective-permute-start.6 = (f32[32,1280]{1,0:T(8,128)S(1)}, f32[32,1280]{1,0:T(8,128)S(1)}, u32[]{:S(2)}, u32[]{:S(2)}) collective-permute-start(f32[32,1280]{1,0:T(8,128)S(1)} %slice.155), channel_id=1, source_target_pairs={{0,1},{1,0},{2,3},{3,2},{4,5},{5,4},{6,7},{7,6},{8,9},{9,8},{10,11... | collective-permute-start | bytes 491528 | tf_op jit(solution)/shard_map/ppermute | solution.py:132
  67.9 21.4 %collective-permute-start.15 = (f32[32,1280]{1,0:T(8,128)S(1)}, f32[32,1280]{1,0:T(8,128)S(1)}, u32[]{:S(2)}, u32[]{:S(2)}) collective-permute-start(f32[32,1280]{1,0:T(8,128)S(1)} %slice.168), channel_id=1, source_target_pairs={{0,1},{1,0},{2,3},{3,2},{4,5},{5,4},{6,7},{7,6},{8,9},{9,8},{10,11... | collective-permute-start | bytes 491528 | tf_op jit(solution)/shard_map/ppermute | solution.py:132
  68.5 12.4 %collective-permute-start.8 = (bf16[64,2560]{1,0:T(8,128)(2,1)S(1)}, bf16[64,2560]{1,0:T(8,128)(2,1)S(1)}, u32[]{:S(2)}, u32[]{:S(2)}) collective-permute-start(bf16[64,2560]{1,0:T(8,128)(2,1)S(1)} %collective-permute-done.5), channel_id=1, source_target_pairs={{0,2},{2,4},{4,6},{6,0},{1,3},{3,5},{5,7},{7,1},{8,10},{10,12},{12... | collective-permute-start | bytes 983048 | tf_op jit(solution)/shard_map/ppermute | solution.py:127
  71.0 14.3 %collective-permute-start.16 = (bf16[64,2560]{1,0:T(8,128)(2,1)S(1)}, bf16[64,2560]{1,0:T(8,128)(2,1)S(1)}, u32[]{:S(2)}, u32[]{:S(2)}) collective-permute-start(bf16[64,2560]{1,0:T(8,128)(2,1)S(1)} %collective-permute-done.14), channel_id=1, source_target_pairs={{0,2},{2,4},{4,6},{6,0},{1,3},{3,5},{5,7},{7,1},{8,10},{10,12},{12... | collective-permute-start | bytes 983048 | tf_op jit(solution)/shard_map/ppermute | solution.py:127
  82.2 6.3 %collective-permute-start.9 = (f32[32,1280]{1,0:T(8,128)S(1)}, f32[32,1280]{1,0:T(8,128)S(1)}, u32[]{:S(2)}, u32[]{:S(2)}) collective-permute-start(f32[32,1280]{1,0:T(8,128)S(1)} %slice.158), channel_id=1, source_target_pairs={{0,1},{1,0},{2,3},{3,2},{4,5},{5,4},{6,7},{7,6},{8,9},{9,8},{10,11... | collective-permute-start | bytes 491528 | tf_op jit(solution)/shard_map/ppermute | solution.py:132
  86.5 5.4 %collective-permute-start.17 = (f32[32,1280]{1,0:T(8,128)S(1)}, f32[32,1280]{1,0:T(8,128)S(1)}, u32[]{:S(2)}, u32[]{:S(2)}) collective-permute-start(f32[32,1280]{1,0:T(8,128)S(1)} %slice.171), channel_id=1, source_target_pairs={{0,1},{1,0},{2,3},{3,2},{4,5},{5,4},{6,7},{7,6},{8,9},{9,8},{10,11... | collective-permute-start | bytes 491528 | tf_op jit(solution)/shard_map/ppermute | solution.py:132
  88.5 12.4 %collective-permute-start.11 = (bf16[128,1280]{1,0:T(8,128)(2,1)S(1)}, bf16[128,1280]{1,0:T(8,128)(2,1)S(1)}, u32[]{:S(2)}, u32[]{:S(2)}) collective-permute-start(bf16[128,1280]{1,0:T(8,128)(2,1)S(1)} %pad_maximum_fusion.1.rest_0_), channel_id=1, source_target_pairs={{0,2},{2,4},{4,6},{6,0},{1,3},{3,5},{5,7},{7,1},{8,10},{10,12},{12... | collective-permute-start | bytes 983048 | tf_op jit(solution)/shard_map/ppermute | solution.py:127
  92.0 15.9 %collective-permute-start.18 = (bf16[128,1280]{1,0:T(8,128)(2,1)S(1)}, bf16[128,1280]{1,0:T(8,128)(2,1)S(1)}, u32[]{:S(2)}, u32[]{:S(2)}) collective-permute-start(bf16[128,1280]{1,0:T(8,128)(2,1)S(1)} %pad_maximum_fusion.3.rest_0_), channel_id=1, source_target_pairs={{0,2},{2,4},{4,6},{6,0},{1,3},{3,5},{5,7},{7,1},{8,10},{10,12},{12... | collective-permute-start | bytes 983048 | tf_op jit(solution)/shard_map/ppermute | solution.py:127
  101.0 14.0 %collective-permute-start.19 = (bf16[128,1280]{1,0:T(8,128)(2,1)S(1)}, bf16[128,1280]{1,0:T(8,128)(2,1)S(1)}, u32[]{:S(2)}, u32[]{:S(2)}) collective-permute-start(bf16[128,1280]{1,0:T(8,128)(2,1)S(1)} %collective-permute-done.11.rest_1_), channel_id=1, source_target_pairs={{0,2},{2,4},{4,6},{6,0},{1,3},{3,5},{5,7},{7,1},{8,10},{10,12},{12... | collective-permute-start | bytes 983048 | tf_op jit(solution)/shard_map/ppermute | solution.py:127
  108.0 14.0 %collective-permute-start.20 = (bf16[128,1280]{1,0:T(8,128)(2,1)S(1)}, bf16[128,1280]{1,0:T(8,128)(2,1)S(1)}, u32[]{:S(2)}, u32[]{:S(2)}) collective-permute-start(bf16[128,1280]{1,0:T(8,128)(2,1)S(1)} %collective-permute-done.18.rest_1_), channel_id=1, source_target_pairs={{0,2},{2,4},{4,6},{6,0},{1,3},{3,5},{5,7},{7,1},{8,10},{10,12},{12... | collective-permute-start | bytes 983048 | tf_op jit(solution)/shard_map/ppermute | solution.py:127
  115.0 13.8 %collective-permute-start.21 = (bf16[128,1280]{1,0:T(8,128)(2,1)S(1)}, bf16[128,1280]{1,0:T(8,128)(2,1)S(1)}, u32[]{:S(2)}, u32[]{:S(2)}) collective-permute-start(bf16[128,1280]{1,0:T(8,128)(2,1)S(1)} %collective-permute-done.19.rest_2_), channel_id=1, source_target_pairs={{0,2},{2,4},{4,6},{6,0},{1,3},{3,5},{5,7},{7,1},{8,10},{10,12},{12... | collective-permute-start | bytes 983048 | tf_op jit(solution)/shard_map/ppermute | solution.py:127
  115.0 16.0 %collective-permute-start.23 = (bf16[128,1280]{1,0:T(8,128)(2,1)S(1)}, bf16[128,1280]{1,0:T(8,128)(2,1)S(1)}, u32[]{:S(2)}, u32[]{:S(2)}) collective-permute-start(bf16[128,1280]{1,0:T(8,128)(2,1)S(1)} %pad_maximum_fusion.1.rest_0_), channel_id=1, source_target_pairs={{0,1},{1,0},{2,3},{3,2},{4,5},{5,4},{6,7},{7,6},{8,9},{9,8},{10,11... | collective-permute-start | bytes 983048 | tf_op jit(solution)/shard_map/ppermute | solution.py:132
  116.6 15.0 %collective-permute-start.24 = (bf16[128,1280]{1,0:T(8,128)(2,1)S(1)}, bf16[128,1280]{1,0:T(8,128)(2,1)S(1)}, u32[]{:S(2)}, u32[]{:S(2)}) collective-permute-start(bf16[128,1280]{1,0:T(8,128)(2,1)S(1)} %collective-permute-done.11.rest_1_), channel_id=1, source_target_pairs={{0,1},{1,0},{2,3},{3,2},{4,5},{5,4},{6,7},{7,6},{8,9},{9,8},{10,11... | collective-permute-start | bytes 983048 | tf_op jit(solution)/shard_map/ppermute | solution.py:132
  117.1 21.3 %collective-permute-start.25 = (bf16[128,1280]{1,0:T(8,128)(2,1)S(1)}, bf16[128,1280]{1,0:T(8,128)(2,1)S(1)}, u32[]{:S(2)}, u32[]{:S(2)}) collective-permute-start(bf16[128,1280]{1,0:T(8,128)(2,1)S(1)} %collective-permute-done.19.rest_2_), channel_id=1, source_target_pairs={{0,1},{1,0},{2,3},{3,2},{4,5},{5,4},{6,7},{7,6},{8,9},{9,8},{10,11... | collective-permute-start | bytes 983048 | tf_op jit(solution)/shard_map/ppermute | solution.py:132
  122.0 17.9 %collective-permute-start.22 = (bf16[128,1280]{1,0:T(8,128)(2,1)S(1)}, bf16[128,1280]{1,0:T(8,128)(2,1)S(1)}, u32[]{:S(2)}, u32[]{:S(2)}) collective-permute-start(bf16[128,1280]{1,0:T(8,128)(2,1)S(1)} %collective-permute-done.20.rest_2_), channel_id=1, source_target_pairs={{0,2},{2,4},{4,6},{6,0},{1,3},{3,5},{5,7},{7,1},{8,10},{10,12},{12... | collective-permute-start | bytes 983048 | tf_op jit(solution)/shard_map/ppermute | solution.py:127
  128.8 16.7 %collective-permute-start.26 = (bf16[128,1280]{1,0:T(8,128)(2,1)S(1)}, bf16[128,1280]{1,0:T(8,128)(2,1)S(1)}, u32[]{:S(2)}, u32[]{:S(2)}) collective-permute-start(bf16[128,1280]{1,0:T(8,128)(2,1)S(1)} %collective-permute-done.21.rest_3_), channel_id=1, source_target_pairs={{0,1},{1,0},{2,3},{3,2},{4,5},{5,4},{6,7},{7,6},{8,9},{9,8},{10,11... | collective-permute-start | bytes 983048 | tf_op jit(solution)/shard_map/ppermute | solution.py:132
  131.0 23.7 %collective-permute-start.27 = (bf16[128,1280]{1,0:T(8,128)(2,1)S(1)}, bf16[128,1280]{1,0:T(8,128)(2,1)S(1)}, u32[]{:S(2)}, u32[]{:S(2)}) collective-permute-start(bf16[128,1280]{1,0:T(8,128)(2,1)S(1)} %pad_maximum_fusion.3.rest_0_), channel_id=1, source_target_pairs={{0,1},{1,0},{2,3},{3,2},{4,5},{5,4},{6,7},{7,6},{8,9},{9,8},{10,11... | collective-permute-start | bytes 983048 | tf_op jit(solution)/shard_map/ppermute | solution.py:132
  131.6 27.8 %collective-permute-start.28 = (bf16[128,1280]{1,0:T(8,128)(2,1)S(1)}, bf16[128,1280]{1,0:T(8,128)(2,1)S(1)}, u32[]{:S(2)}, u32[]{:S(2)}) collective-permute-start(bf16[128,1280]{1,0:T(8,128)(2,1)S(1)} %collective-permute-done.18.rest_1_), channel_id=1, source_target_pairs={{0,1},{1,0},{2,3},{3,2},{4,5},{5,4},{6,7},{7,6},{8,9},{9,8},{10,11... | collective-permute-start | bytes 983048 | tf_op jit(solution)/shard_map/ppermute | solution.py:132
  138.5 24.5 %collective-permute-start.29 = (bf16[128,1280]{1,0:T(8,128)(2,1)S(1)}, bf16[128,1280]{1,0:T(8,128)(2,1)S(1)}, u32[]{:S(2)}, u32[]{:S(2)}) collective-permute-start(bf16[128,1280]{1,0:T(8,128)(2,1)S(1)} %collective-permute-done.20.rest_2_), channel_id=1, source_target_pairs={{0,1},{1,0},{2,3},{3,2},{4,5},{5,4},{6,7},{7,6},{8,9},{9,8},{10,11... | collective-permute-start | bytes 983048 | tf_op jit(solution)/shard_map/ppermute | solution.py:132
  140.0 26.5 %collective-permute-start.30 = (bf16[128,1280]{1,0:T(8,128)(2,1)S(1)}, bf16[128,1280]{1,0:T(8,128)(2,1)S(1)}, u32[]{:S(2)}, u32[]{:S(2)}) collective-permute-start(bf16[128,1280]{1,0:T(8,128)(2,1)S(1)} %collective-permute-done.22.rest_3_), channel_id=1, source_target_pairs={{0,1},{1,0},{2,3},{3,2},{4,5},{5,4},{6,7},{7,6},{8,9},{9,8},{10,11... | collective-permute-start | bytes 983048 | tf_op jit(solution)/shard_map/ppermute | solution.py:132
  177.8 12.2 %all-to-all-start = ((f32[8,1,192]{2,1,0:T(1,128)}), f32[8,1,192]{2,1,0:T(1,128)S(1)}, u32[]{:S(2)}, u32[]{:S(2)}) async-start(f32[8,1,192]{2,1,0:T(1,128)} %reshape.113), calls=%async_computation | async-start | bytes 16384 | tf_op jit(solution)/shard_map/all_to_all | solution.py:226
  (11 other events, 198.7 us)

commit v2 on v1

v2 whole, which is shorter than its diff:
```python
import functools

import jax
import jax.numpy as jnp
from jax import lax
from jax.experimental import pallas as pl
from jax.experimental.pallas import tpu as pltpu
from jax.sharding import PartitionSpec as P


EPSILON = 1e-06
VMEM = pl.BlockSpec(memory_space=pltpu.VMEM)
SMEM = pl.BlockSpec(memory_space=pltpu.SMEM)


def halves(local_rows):
    return 2 if local_rows % 64 == 0 else 1


def ahead(value, shift, count):
    moved = value + shift
    return jnp.where(moved >= count, moved - count, moved)


def behind(value, shift, count):
    moved = value - shift
    return jnp.where(moved < 0, moved + count, moved)


def stream_kernel(shape, part, where_ref, *refs):
    dp_count, tensor_count, rows = shape
    partials, refs = refs[:dp_count], refs[dp_count:]
    residuals, refs = refs[:dp_count], refs[dp_count:]
    received, out_ref = refs[:-1], refs[-1]
    first = pl.multiple_of(where_ref[1] * rows, rows)
    for s in range(dp_count):
        total = partials[s][pl.ds(first, rows), :]
        for j in range(tensor_count - 1):
            total = total + received[s * (tensor_count - 1) + j][...]
        mine = residuals[s][part * rows : (part + 1) * rows, :].astype(jnp.float32)
        out_ref[s * rows : (s + 1) * rows, :] = (mine + total).astype(jnp.bfloat16)


def stream_block(where, partials, residuals, received, shape, part):
    dp_count, _, rows = shape
    columns = residuals[0].shape[1]
    return pl.pallas_call(
        functools.partial(stream_kernel, shape, part),
        in_specs=[SMEM] + [VMEM] * (2 * dp_count + len(received)),
        out_specs=VMEM,
        out_shape=jax.ShapeDtypeStruct((dp_count * rows, columns), jnp.bfloat16),
        compiler_params=pltpu.CompilerParams(vmem_limit_bytes=16 * 1024 * 1024),
        cost_estimate=pl.CostEstimate(
            flops=100_000_000, bytes_accessed=12 * dp_count * rows * columns, transcendentals=0
        ),
    )(where, *partials, *residuals, *received)


def head_kernel(shape, where_ref, wanted_ref, earlier_ref, gain_ref, weight_ref, *rest):
    dp_count, tensor_count, rows, columns, vocab, part = shape
    devices = dp_count * tensor_count
    blocks = rest[:devices]
    out_ref, normed_ref, stats_ref = rest[devices:]
    step = pl.program_id(0)

    @pl.when(step == 0)
    def _():
        for j in range(tensor_count):
            tensor = behind(where_ref[1], j, tensor_count)
            for rho in range(dp_count):
                taken = []
                squares = jnp.zeros((rows, 1), jnp.float32)
                for k in range(dp_count):
                    s = (rho - k) % dp_count
                    value = blocks[j * dp_count + k][s * rows : (s + 1) * rows, :]
                    value = value.astype(jnp.float32)
                    squares = squares + jnp.sum(value * value, axis=1, keepdims=True)
                    taken.append(value)
                scale = lax.rsqrt(squares / (dp_count * columns) + EPSILON)
                owner = behind(where_ref[0], rho, dp_count) * tensor_count + tensor
                first = pl.multiple_of(owner * rows, rows)
                for k, value in enumerate(taken):
                    at = pl.multiple_of(behind(where_ref[0], k, dp_count) * columns, columns)
                    gain = gain_ref[:, pl.ds(at, columns)]
                    normed_ref[pl.ds(first, rows), pl.ds(at, columns)] = (
                        value * scale * gain
                    ).astype(jnp.bfloat16)
        count = devices * rows
        stats_ref[0:1, :] = jnp.full((1, count), -jnp.inf, jnp.float32)
        stats_ref[1:3, :] = jnp.zeros((2, count), jnp.float32)

    logits = lax.dot_general(
        weight_ref[...],
        normed_ref[...],
        (((1,), (1,)), ((), ())),
        preferred_element_type=jnp.float32,
    )
    entry = lax.broadcasted_iota(jnp.int32, logits.shape, 0) + step * logits.shape[0]
    masked = jnp.where(entry < vocab, logits, -jnp.inf)
    before = stats_ref[0:1, :]
    highest = jnp.maximum(before, jnp.max(masked, axis=0, keepdims=True))
    stats_ref[1:2, :] = stats_ref[1:2, :] * jnp.exp(before - highest) + jnp.sum(
        jnp.exp(masked - highest), axis=0, keepdims=True
    )
    stats_ref[0:1, :] = highest
    hit = jnp.logical_and(entry == wanted_ref[...], entry < vocab)
    stats_ref[2:3, :] = stats_ref[2:3, :] + jnp.sum(
        jnp.where(hit, logits, 0.0), axis=0, keepdims=True
    )

    @pl.when(step == pl.num_programs(0) - 1)
    def _():
        done = 3 * rows * part
        if part:
            out_ref[:, :, :done] = earlier_ref[...]
        for owner in range(devices):
            for item in range(3):
                out_ref[owner, :, done + item * rows : done + (item + 1) * rows] = stats_ref[
                    item : item + 1, owner * rows : (owner + 1) * rows
                ]


def head_stats(blocks, where, wanted, earlier, norm_gain, head_weight, shape):
    dp_count, tensor_count, rows, columns, vocab, part = shape
    devices = dp_count * tensor_count
    count = devices * rows
    width = dp_count * columns
    entries = -(-vocab // (5 * 16)) * 16
    steps = -(-vocab // entries)
    return pl.pallas_call(
        functools.partial(head_kernel, shape),
        grid=(steps,),
        in_specs=[
            SMEM,
            pl.BlockSpec((1, count), lambda i: (0, 0)),
            VMEM,
            pl.BlockSpec((1, width), lambda i: (0, 0)),
            pl.BlockSpec((entries, width), lambda i: (i, 0)),
        ]
        + [VMEM] * len(blocks),
        out_specs=VMEM,
        out_shape=jax.ShapeDtypeStruct((devices, 1, 3 * rows * (part + 1)), jnp.float32),
        scratch_shapes=[
            pltpu.VMEM((count, width), jnp.bfloat16),
            pltpu.VMEM((8, count), jnp.float32),
        ],
        compiler_params=pltpu.CompilerParams(
            dimension_semantics=("arbitrary",), vmem_limit_bytes=40 * 1024 * 1024
        ),
        cost_estimate=pl.CostEstimate(
            flops=2 * count * width * vocab,
            bytes_accessed=2 * vocab * width + 4 * count * width,
            transcendentals=count * vocab,
        ),
    )(where, wanted, earlier, norm_gain, head_weight, *blocks)


def loss_kernel(rows, parts, table_ref, out_ref):
    for h in range(parts):
        base = 3 * rows * h
        highest = table_ref[:, 0, base : base + rows]
        summed = table_ref[:, 0, base + rows : base + 2 * rows]
        picked = table_ref[:, 0, base + 2 * rows : base + 3 * rows]
        top = jnp.max(highest, axis=0, keepdims=True)
        total = jnp.sum(summed * jnp.exp(highest - top), axis=0, keepdims=True)
        loss = jnp.log(total) + top - jnp.sum(picked, axis=0, keepdims=True)
        out_ref[:, rows * h : rows * (h + 1)] = loss


def local(context, out_weight, residual, norm_gain, head_weight, targets):
    dp_count = lax.axis_size("dp")
    tensor_count = lax.axis_size("tensor")
    d = lax.axis_index("dp")
    t = lax.axis_index("tensor")
    where = jnp.stack([d, t]).astype(jnp.int32)
    local_rows, width = residual.shape
    parts = halves(local_rows)
    rows = local_rows // parts
    depth = context.shape[1]
    columns = out_weight.shape[1]
    vocab = head_weight.shape[0]
    devices = dp_count * tensor_count
    vocab_start = (d * tensor_count + t) * vocab

    def along_dp(value, shift):
        return lax.ppermute(
            value, "dp", [(i, (i + shift) % dp_count) for i in range(dp_count)]
        )

    def along_tensor(value, shift):
        return lax.ppermute(
            value, "tensor", [(i, (i + shift) % tensor_count) for i in range(tensor_count)]
        )

    residuals = []
    for s in range(dp_count):
        cut = lax.dynamic_slice(
            residual, (0, ahead(d, s, dp_count) * columns), (local_rows, columns)
        )
        residuals.append(along_dp(cut, s) if s else cut)

    by_tensor = context.reshape(tensor_count, parts, rows, depth)
    shape = (dp_count, tensor_count, rows)
    gathered = []
    for h in range(parts):
        held = by_tensor[:, h].reshape(tensor_count * rows, depth)
        partials, received = [], []
        for s in range(dp_count):
            if s:
                held = along_dp(held, 1)
            partial = jnp.dot(held, out_weight, preferred_element_type=jnp.float32)
            partials.append(partial)
            for j in range(1, tensor_count):
                other = lax.dynamic_slice(
                    partial, (ahead(t, j, tensor_count) * rows, 0), (rows, columns)
                )
                received.append(along_tensor(other, j))
        block = stream_block(where, partials, residuals, received, shape, h)
        arrived = []
        for k in range(dp_count):
            if k:
                block = along_dp(block, 1)
            if h == parts - 1 and k == dp_count - 1:
                others = [along_dp(arrived[-1][j], 1) for j in range(1, tensor_count)]
            else:
                others = [along_tensor(block, j) for j in range(1, tensor_count)]
            arrived.append([block] + others)
        gathered.append(arrived)

    stream = jnp.zeros((local_rows, width), jnp.bfloat16)
    for k in range(dp_count):
        s = (dp_count - k) % dp_count
        piece = jnp.concatenate(
            [gathered[h][k][0][s * rows : (s + 1) * rows] for h in range(parts)], axis=0
        )
        stream = lax.dynamic_update_slice(stream, piece, (0, behind(d, k, dp_count) * columns))

    wanted = targets.reshape(devices, parts, rows) - vocab_start
    table = jnp.zeros((devices, 1, 128), jnp.float32)
    for h in range(parts):
        blocks = [gathered[h][k][j] for j in range(tensor_count) for k in range(dp_count)]
        table = head_stats(
            blocks,
            where,
            wanted[:, h].reshape(1, devices * rows),
            table,
            norm_gain[None, :],
            head_weight,
            (dp_count, tensor_count, rows, columns, vocab, h),
        )

    table = lax.all_to_all(table, ("dp", "tensor"), 0, 0, tiled=True)
    token_loss = pl.pallas_call(
        functools.partial(loss_kernel, rows, parts),
        in_specs=[VMEM],
        out_specs=VMEM,
        out_shape=jax.ShapeDtypeStruct((1, local_rows), jnp.float32),
        compiler_params=pltpu.CompilerParams(vmem_limit_bytes=4 * 1024 * 1024),
        name="loss",
    )(table).reshape(local_rows)
    return (stream, token_loss)


def solution(mesh):
    def program(context, out_weight, residual, norm_gain, head_weight, targets):
        step = jax.shard_map(
            local,
            mesh=mesh,
            in_specs=(
                P(("member", "dp"), "tensor"),
                P(("member", "tensor"), "dp"),
                P(("member", "dp", "tensor"), None),
                P("member"),
                P(("member", "dp", "tensor"), None),
                P("member"),
            ),
            out_specs=(P(("member", "dp", "tensor"), None), P(("member", "dp", "tensor"))),
            check_vma=False,
        )
        return step(context, out_weight, residual, norm_gain, head_weight, targets)

    return program
```

time: 192 us -> 176 us (0.917)
  starting transfers between devices: 44 us -> 32.3 us
  other arithmetic: 9.12 us -> 0.14 us
  waiting for transfers between devices: 90.7 us -> 99.5 us
  local copies, waits for them, and re-layouts: 10 us -> 3.36 us
  Pallas kernels: 18.2 us -> 21 us
    ppermute x15 -> x16, starting transfers between devices: 19.3 us -> 10.4 us  [along_dp(): lax.ppermute(value, 'dp', [(i, (i + shift) % dp_count) for i in range(dp_...]
    ppermute x16 -> x15, waiting for transfers between devices: 24.4 us -> 29 us  [along_tensor(): lax.ppermute(value, 'tensor', [(i, (i + shift) % tensor_count) for i in r...]
    ppermute x15 -> x16, waiting for transfers between devices: 60.5 us -> 64 us  [along_dp(): lax.ppermute(value, 'dp', [(i, (i + shift) % dp_count) for i in range(dp_...]
    convert_element_type x8 -> x0, other arithmetic: 3.37 us -> none  [local(): pieces.append((mine + total).astype(jnp.bfloat16))]
    slice x21 -> x10, local copies, waits for them, and re-layouts: 4.48 us -> 1.2 us  [the longest x1 1.12 us: local(): held = by_tensor[:, h].reshape(tensor_count * rows, depth)]
    dynamic_update_slice x4, other arithmetic: 2.71 us -> 0.06 us  [local(): lax.dynamic_update_slice(stream, piece, (0, behind(d, k, dp_count) * colu...]
    pallas_call x0 -> x3, Pallas kernels: none -> 2 us  [the longest x2 1.33 us: stream_block(): pl.pallas_call(functools.partial(stream_kernel, shape, part), in_specs=[S...]
    ppermute x16 -> x15, starting transfers between devices: 18.9 us -> 17.3 us  [along_tensor(): lax.ppermute(value, 'tensor', [(i, (i + shift) % tensor_count) for i in r...]
  transfers between devices with their start and end apart: 32 -> 32, of which waited for: 18 -> 22; matrix products, arithmetic and copies ran while one was open for 14% -> 12% of each run, Pallas kernels for 5% -> 6%
where the time goes in v2:
time: 176 us
  waiting for transfers between devices  99.5 us (57%)
  starting transfers between devices  32.3 us (18%)
  Pallas kernels  21 us (12%)
  matrix products  18.7 us (11%)
  local copies, waits for them, and re-layouts  3.36 us (2%)
    ppermute x16, waiting for transfers between devices, along_dp(): lax.ppermute(value, 'dp', [(i, (i + shift) % dp_count) for i in range(dp_...  64 us
    ppermute x15, waiting for transfers between devices, along_tensor(): lax.ppermute(value, 'tensor', [(i, (i + shift) % tensor_count) for i in r...  29 us
    pallas_call x2, Pallas kernels, head_stats(): pl.pallas_call(functools.partial(head_kernel, shape), grid=(steps,), in_s...  19 us
    dot_general x8, matrix products, local(): partial = jnp.dot(held, out_weight, preferred_element_type=jnp.float32)  18.7 us
    ppermute x15, starting transfers between devices, along_tensor(): lax.ppermute(value, 'tensor', [(i, (i + shift) % tensor_count) for i in r...  17.3 us
    ppermute x16, starting transfers between devices, along_dp(): lax.ppermute(value, 'dp', [(i, (i + shift) % dp_count) for i in range(dp_...  10.4 us
    all_to_all x1, waiting for transfers between devices, local(): table = lax.all_to_all(table, ('dp', 'tensor'), 0, 0, tiled=True)  6.49 us
    all_to_all x1, starting transfers between devices, local(): table = lax.all_to_all(table, ('dp', 'tensor'), 0, 0, tiled=True)  4.65 us
  transfers between devices with their start and end apart: 32, of which 22 were waited for; matrix products, arithmetic and copies ran while one was open for 12% of the time, Pallas kernels for 6%

profile of v2, /device:TPU:0, one launch (start us, length us, event | category | flops | bytes accessed | tf_op | source)
XLA Modules:
  0.0 176.1 jit_solution(2826614721318615750)
XLA Ops:
  1.9 3.1 %collective-permute-start.3 = (bf16[64,1280]{1,0:T(8,128)(2,1)S(1)}, bf16[64,1280]{1,0:T(8,128)(2,1)S(1)}, u32[]{:S(2)}, u32[]{:S(2)}) collective-permute-start(bf16[64,1280]{1,0:T(8,128)(2,1)S(1)} %get-tuple-element.7), channel_id=1, source_target_pairs={{0,2},{2,4},{4,6},{6,0},{1,3},{3,5},{5,7},{7,1},{8,10},{10,12},{12... | collective-permute-start | bytes 491528 | tf_op jit(solution)/shard_map/ppermute | solution.py:186
  5.0 2.6 %collective-permute-start.4 = (bf16[64,1280]{1,0:T(8,128)(2,1)S(1)}, bf16[64,1280]{1,0:T(8,128)(2,1)S(1)}, u32[]{:S(2)}, u32[]{:S(2)}) collective-permute-start(bf16[64,1280]{1,0:T(8,128)(2,1)S(1)} %get-tuple-element.9), channel_id=1, source_target_pairs={{0,4},{2,6},{4,0},{6,2},{1,5},{3,7},{5,1},{7,3},{8,12},{10,14},{12... | collective-permute-start | bytes 491528 | tf_op jit(solution)/shard_map/ppermute | solution.py:186
  10.9 4.3 %fusion.1.refs_0_ = f32[64,1280]{1,0:T(8,128)S(1)} fusion(bf16[64,2560]{1,0:T(8,128)(2,1)S(1)} %bitcast.30, bf16[2560,1280]{1,0:T(8,128)(2,1)} %param.7), kind=kOutput, calls=%fused_computation.21 | convolution fusion | flops 419430400 | bytes 7208960 | tf_op jit(solution)/shard_map/dot_general | solution.py:211
  16.9 9.3 %collective-permute-done = bf16[64,2560]{1,0:T(8,128)(2,1)S(1)} collective-permute-done((bf16[64,2560]{1,0:T(8,128)(2,1)S(1)}, bf16[64,2560]{1,0:T(8,128)(2,1)S(1)}, u32[]{:S(2)}, u32[]{:S(2)}) %collective-permute-start) | collective-permute-done | bytes 327712 | tf_op jit(solution)/shard_map/ppermute | solution.py:186
  26.3 1.7 collective-permute-start.6
  28.0 4.1 %fusion.2.refs_1_ = f32[64,1280]{1,0:T(8,128)S(1)} fusion(bf16[64,2560]{1,0:T(8,128)(2,1)S(1)} %collective-permute-done, bf16[2560,1280]{1,0:T(8,128)(2,1)} %param.7), kind=kOutput, calls=%fused_computation.22 | convolution fusion | flops 419430400 | bytes 7208960 | tf_op jit(solution)/shard_map/dot_general | solution.py:211
  32.4 2.2 %collective-permute-start.1 = (bf16[64,2560]{1,0:T(8,128)(2,1)S(1)}, bf16[64,2560]{1,0:T(8,128)(2,1)S(1)}, u32[]{:S(2)}, u32[]{:S(2)}) collective-permute-start(bf16[64,2560]{1,0:T(8,128)(2,1)S(1)} %collective-permute-done), channel_id=1, source_target_pairs={{0,2},{2,4},{4,6},{6,0},{1,3},{3,5},{5,7},{7,1},{8,10},{10,12},{12... | collective-permute-start | bytes 983048 | tf_op jit(solution)/shard_map/ppermute | solution.py:186
  34.7 4.1 %fusion.6.refs_1_ = f32[64,1280]{1,0:T(8,128)S(1)} fusion(bf16[64,2560]{1,0:T(8,128)(2,1)S(1)} %collective-permute-done.10, bf16[2560,1280]{1,0:T(8,128)(2,1)} %param.7), kind=kOutput, calls=%fused_computation.26 | convolution fusion | flops 419430400 | bytes 7208960 | tf_op jit(solution)/shard_map/dot_general | solution.py:211
  38.8 4.2 %collective-permute-done.1 = bf16[64,2560]{1,0:T(8,128)(2,1)S(1)} collective-permute-done((bf16[64,2560]{1,0:T(8,128)(2,1)S(1)}, bf16[64,2560]{1,0:T(8,128)(2,1)S(1)}, u32[]{:S(2)}, u32[]{:S(2)}) %collective-permute-start.1) | collective-permute-done | bytes 327712 | tf_op jit(solution)/shard_map/ppermute | solution.py:186
  44.5 8.3 %collective-permute-done.11 = bf16[64,2560]{1,0:T(8,128)(2,1)S(1)} collective-permute-done((bf16[64,2560]{1,0:T(8,128)(2,1)S(1)}, bf16[64,2560]{1,0:T(8,128)(2,1)S(1)}, u32[]{:S(2)}, u32[]{:S(2)}) %collective-permute-start.11) | collective-permute-done | bytes 327712 | tf_op jit(solution)/shard_map/ppermute | solution.py:186
  54.1 7.6 %collective-permute-done.2 = bf16[64,2560]{1,0:T(8,128)(2,1)S(1)} collective-permute-done((bf16[64,2560]{1,0:T(8,128)(2,1)S(1)}, bf16[64,2560]{1,0:T(8,128)(2,1)S(1)}, u32[]{:S(2)}, u32[]{:S(2)}) %collective-permute-start.2) | collective-permute-done | bytes 327712 | tf_op jit(solution)/shard_map/ppermute | solution.py:186
  63.0 7.6 %collective-permute-done.12 = bf16[64,2560]{1,0:T(8,128)(2,1)S(1)} collective-permute-done((bf16[64,2560]{1,0:T(8,128)(2,1)S(1)}, bf16[64,2560]{1,0:T(8,128)(2,1)S(1)}, u32[]{:S(2)}, u32[]{:S(2)}) %collective-permute-start.12) | collective-permute-done | bytes 327712 | tf_op jit(solution)/shard_map/ppermute | solution.py:186
  78.7 2.5 %collective-permute-done.8.refs_10_ = f32[32,1280]{1,0:T(8,128)S(1)} collective-permute-done((f32[32,1280]{1,0:T(8,128)S(1)}, f32[32,1280]{1,0:T(8,128)S(1)}, u32[]{:S(2)}, u32[]{:S(2)}) %collective-permute-start.8) | collective-permute-done | bytes 163872 | tf_op jit(solution)/shard_map/ppermute | solution.py:191
  82.3 2.4 %collective-permute-done.9.refs_11_ = f32[32,1280]{1,0:T(8,128)S(1)} collective-permute-done((f32[32,1280]{1,0:T(8,128)S(1)}, f32[32,1280]{1,0:T(8,128)S(1)}, u32[]{:S(2)}, u32[]{:S(2)}) %collective-permute-start.9) | collective-permute-done | bytes 163872 | tf_op jit(solution)/shard_map/ppermute | solution.py:191
  85.4 2.6 %collective-permute-done.13.refs_8_ = f32[32,1280]{1,0:T(8,128)S(1)} collective-permute-done((f32[32,1280]{1,0:T(8,128)S(1)}, f32[32,1280]{1,0:T(8,128)S(1)}, u32[]{:S(2)}, u32[]{:S(2)}) %collective-permute-start.13) | collective-permute-done | bytes 163872 | tf_op jit(solution)/shard_map/ppermute | solution.py:191
  88.0 1.8 collective-permute-done.14.refs_9_
  89.7 1.8 collective-permute-done.15.refs_10_
  91.5 1.8 collective-permute-done.16.refs_11_
  94.0 1.5 collective-permute-done.17.rest_1_
  95.5 10.8 %collective-permute-done.18.rest_1_ = bf16[128,1280]{1,0:T(8,128)(2,1)S(1)} collective-permute-done((bf16[128,1280]{1,0:T(8,128)(2,1)S(1)}, bf16[128,1280]{1,0:T(8,128)(2,1)S(1)}, u32[]{:S(2)}, u32[]{:S(2)}) %collective-permute-start.18) | collective-permute-done | bytes 327712 | tf_op jit(solution)/shard_map/ppermute | solution.py:186
  106.5 1.4 collective-permute-start.23
  107.8 5.6 %collective-permute-done.19.rest_2_ = bf16[128,1280]{1,0:T(8,128)(2,1)S(1)} collective-permute-done((bf16[128,1280]{1,0:T(8,128)(2,1)S(1)}, bf16[128,1280]{1,0:T(8,128)(2,1)S(1)}, u32[]{:S(2)}, u32[]{:S(2)}) %collective-permute-start.19) | collective-permute-done | bytes 327712 | tf_op jit(solution)/shard_map/ppermute | solution.py:186
  113.6 1.4 collective-permute-start.24
  115.0 5.4 %collective-permute-done.20.rest_2_ = bf16[128,1280]{1,0:T(8,128)(2,1)S(1)} collective-permute-done((bf16[128,1280]{1,0:T(8,128)(2,1)S(1)}, bf16[128,1280]{1,0:T(8,128)(2,1)S(1)}, u32[]{:S(2)}, u32[]{:S(2)}) %collective-permute-start.20) | collective-permute-done | bytes 327712 | tf_op jit(solution)/shard_map/ppermute | solution.py:186
  122.6 3.3 %collective-permute-done.21.rest_3_ = bf16[128,1280]{1,0:T(8,128)(2,1)S(1)} collective-permute-done((bf16[128,1280]{1,0:T(8,128)(2,1)S(1)}, bf16[128,1280]{1,0:T(8,128)(2,1)S(1)}, u32[]{:S(2)}, u32[]{:S(2)}) %collective-permute-start.21) | collective-permute-done | bytes 327712 | tf_op jit(solution)/shard_map/ppermute | solution.py:186
  128.0 3.2 %collective-permute-done.29.rest_6_ = bf16[128,1280]{1,0:T(8,128)(2,1)S(1)} collective-permute-done((bf16[128,1280]{1,0:T(8,128)(2,1)S(1)}, bf16[128,1280]{1,0:T(8,128)(2,1)S(1)}, u32[]{:S(2)}, u32[]{:S(2)}) %collective-permute-start.29) | collective-permute-done | bytes 327712 | tf_op jit(solution)/shard_map/ppermute | solution.py:191
  132.7 5.6 %collective-permute-done.25.rest_6_ = bf16[128,1280]{1,0:T(8,128)(2,1)S(1)} collective-permute-done((bf16[128,1280]{1,0:T(8,128)(2,1)S(1)}, bf16[128,1280]{1,0:T(8,128)(2,1)S(1)}, u32[]{:S(2)}, u32[]{:S(2)}) %collective-permute-start.25) | collective-permute-done | bytes 327712 | tf_op jit(solution)/shard_map/ppermute | solution.py:191
  138.3 6.8 %collective-permute-done.26.rest_7_ = bf16[128,1280]{1,0:T(8,128)(2,1)S(1)} collective-permute-done((bf16[128,1280]{1,0:T(8,128)(2,1)S(1)}, bf16[128,1280]{1,0:T(8,128)(2,1)S(1)}, u32[]{:S(2)}, u32[]{:S(2)}) %collective-permute-start.26) | collective-permute-done | bytes 327712 | tf_op jit(solution)/shard_map/ppermute | solution.py:191
  145.1 9.2 %shard_map.79.earlier_ref = f32[8,1,96]{2,1,0:T(1,128)S(1)} custom-call(s32[2]{0:T(128)S(1)} %pad_add_fusion.where_ref, s32[1,256]{1,0:T(1,128)S(1)} %reshape_squeeze.15.wanted_ref, f32[8,1,128]{2,1,0:T(1,128)S(1)} %broadcast_in_dim.11.earlier_ref, f32[1,5120]{1,0:T(1,128)S(1)} %bitcast.23, bf16[1188,5120]{1,0:T(8,128)(2,1)} %weight_ref.3, ...), custom_call_target="tpu_custom_call" | custom-call | flops 3114270720 | bytes 17408000 | tf_op jit(solution)/shard_map/pallas_call | solution.py:130
  154.4 9.8 %shard_map.80 = f32[8,1,192]{2,1,0:T(1,128)} custom-call(s32[2]{0:T(128)S(1)} %pad_add_fusion.where_ref, s32[1,256]{1,0:T(1,128)S(1)} %reshape_squeeze.14.wanted_ref, f32[8,1,96]{2,1,0:T(1,128)S(1)} %shard_map.79.earlier_ref, f32[1,5120]{1,0:T(1,128)S(1)} %bitcast.24, bf16[1188,5120]{1,0:T(8,128)(2,1)} %weight_ref.3, ...), custom_call_target="tpu_custom_call" | custom-call | flops 3114270720 | bytes 17408000 | tf_op jit(solution)/shard_map/pallas_call | solution.py:130
  164.2 4.7 %all-to-all-start = ((f32[8,1,192]{2,1,0:T(1,128)}), f32[8,1,192]{2,1,0:T(1,128)S(1)}, u32[]{:S(2)}, u32[]{:S(2)}) async-start(f32[8,1,192]{2,1,0:T(1,128)} %shard_map.80), calls=%async_computation | async-start | bytes 16384 | tf_op jit(solution)/shard_map/all_to_all | solution.py:252
  168.9 6.5 %all-to-all-done.table_ref = f32[8,1,192]{2,1,0:T(1,128)S(1)} async-done(((f32[8,1,192]{2,1,0:T(1,128)}), f32[8,1,192]{2,1,0:T(1,128)S(1)}, u32[]{:S(2)}, u32[]{:S(2)}) %all-to-all-start) | async-done | bytes 6176 | tf_op jit(solution)/shard_map/all_to_all | solution.py:252
  (88 shorter events, 27.9 us)
Async XLA Ops:
  1.9 71.0 %collective-permute-start.3 = (bf16[64,1280]{1,0:T(8,128)(2,1)S(1)}, bf16[64,1280]{1,0:T(8,128)(2,1)S(1)}, u32[]{:S(2)}, u32[]{:S(2)}) collective-permute-start(bf16[64,1280]{1,0:T(8,128)(2,1)S(1)} %get-tuple-element.7), channel_id=1, source_target_pairs={{0,2},{2,4},{4,6},{6,0},{1,3},{3,5},{5,7},{7,1},{8,10},{10,12},{12... | collective-permute-start | bytes 491528 | tf_op jit(solution)/shard_map/ppermute | solution.py:186
  5.0 69.0 %collective-permute-start.4 = (bf16[64,1280]{1,0:T(8,128)(2,1)S(1)}, bf16[64,1280]{1,0:T(8,128)(2,1)S(1)}, u32[]{:S(2)}, u32[]{:S(2)}) collective-permute-start(bf16[64,1280]{1,0:T(8,128)(2,1)S(1)} %get-tuple-element.9), channel_id=1, source_target_pairs={{0,4},{2,6},{4,0},{6,2},{1,5},{3,7},{5,1},{7,3},{8,12},{10,14},{12... | collective-permute-start | bytes 491528 | tf_op jit(solution)/shard_map/ppermute | solution.py:186
  7.6 67.4 %collective-permute-start.5 = (bf16[64,1280]{1,0:T(8,128)(2,1)S(1)}, bf16[64,1280]{1,0:T(8,128)(2,1)S(1)}, u32[]{:S(2)}, u32[]{:S(2)}) collective-permute-start(bf16[64,1280]{1,0:T(8,128)(2,1)S(1)} %get-tuple-element.6), channel_id=1, source_target_pairs={{0,6},{2,0},{4,2},{6,4},{1,7},{3,1},{5,3},{7,5},{8,14},{10,8},{12,... | collective-permute-start | bytes 491528 | tf_op jit(solution)/shard_map/ppermute | solution.py:186
  10.0 16.2 %collective-permute-start = (bf16[64,2560]{1,0:T(8,128)(2,1)S(1)}, bf16[64,2560]{1,0:T(8,128)(2,1)S(1)}, u32[]{:S(2)}, u32[]{:S(2)}) collective-permute-start(bf16[64,2560]{1,0:T(8,128)(2,1)S(1)} %bitcast.29), channel_id=1, source_target_pairs={{0,2},{2,4},{4,6},{6,0},{1,3},{3,5},{5,7},{7,1},{8,10},{10,12},{12... | collective-permute-start | bytes 983048 | tf_op jit(solution)/shard_map/ppermute | solution.py:186
  10.8 21.6 %collective-permute-start.10 = (bf16[64,2560]{1,0:T(8,128)(2,1)S(1)}, bf16[64,2560]{1,0:T(8,128)(2,1)S(1)}, u32[]{:S(2)}, u32[]{:S(2)}) collective-permute-start(bf16[64,2560]{1,0:T(8,128)(2,1)S(1)} %bitcast.27), channel_id=1, source_target_pairs={{0,2},{2,4},{4,6},{6,0},{1,3},{3,5},{5,7},{7,1},{8,10},{10,12},{12... | collective-permute-start | bytes 983048 | tf_op jit(solution)/shard_map/ppermute | solution.py:186
  26.3 49.8 %collective-permute-start.6 = (f32[32,1280]{1,0:T(8,128)S(1)}, f32[32,1280]{1,0:T(8,128)S(1)}, u32[]{:S(2)}, u32[]{:S(2)}) collective-permute-start(f32[32,1280]{1,0:T(8,128)S(1)} %constant_dynamic-slice_fusion.7), channel_id=1, source_target_pairs={{0,1},{1,0},{2,3},{3,2},{4,5},{5,4},{6,7},{7,6},{8,9},{9,8},{10,11... | collective-permute-start | bytes 491528 | tf_op jit(solution)/shard_map/ppermute | solution.py:191
  32.4 10.6 %collective-permute-start.1 = (bf16[64,2560]{1,0:T(8,128)(2,1)S(1)}, bf16[64,2560]{1,0:T(8,128)(2,1)S(1)}, u32[]{:S(2)}, u32[]{:S(2)}) collective-permute-start(bf16[64,2560]{1,0:T(8,128)(2,1)S(1)} %collective-permute-done), channel_id=1, source_target_pairs={{0,2},{2,4},{4,6},{6,0},{1,3},{3,5},{5,7},{7,1},{8,10},{10,12},{12... | collective-permute-start | bytes 983048 | tf_op jit(solution)/shard_map/ppermute | solution.py:186
  43.0 9.8 %collective-permute-start.11 = (bf16[64,2560]{1,0:T(8,128)(2,1)S(1)}, bf16[64,2560]{1,0:T(8,128)(2,1)S(1)}, u32[]{:S(2)}, u32[]{:S(2)}) collective-permute-start(bf16[64,2560]{1,0:T(8,128)(2,1)S(1)} %collective-permute-done.10), channel_id=1, source_target_pairs={{0,2},{2,4},{4,6},{6,0},{1,3},{3,5},{5,7},{7,1},{8,10},{10,12},{12... | collective-permute-start | bytes 983048 | tf_op jit(solution)/shard_map/ppermute | solution.py:186
  52.8 8.9 %collective-permute-start.2 = (bf16[64,2560]{1,0:T(8,128)(2,1)S(1)}, bf16[64,2560]{1,0:T(8,128)(2,1)S(1)}, u32[]{:S(2)}, u32[]{:S(2)}) collective-permute-start(bf16[64,2560]{1,0:T(8,128)(2,1)S(1)} %collective-permute-done.1), channel_id=1, source_target_pairs={{0,2},{2,4},{4,6},{6,0},{1,3},{3,5},{5,7},{7,1},{8,10},{10,12},{12... | collective-permute-start | bytes 983048 | tf_op jit(solution)/shard_map/ppermute | solution.py:186
  61.7 8.9 %collective-permute-start.12 = (bf16[64,2560]{1,0:T(8,128)(2,1)S(1)}, bf16[64,2560]{1,0:T(8,128)(2,1)S(1)}, u32[]{:S(2)}, u32[]{:S(2)}) collective-permute-start(bf16[64,2560]{1,0:T(8,128)(2,1)S(1)} %collective-permute-done.11), channel_id=1, source_target_pairs={{0,2},{2,4},{4,6},{6,0},{1,3},{3,5},{5,7},{7,1},{8,10},{10,12},{12... | collective-permute-start | bytes 983048 | tf_op jit(solution)/shard_map/ppermute | solution.py:186
  70.6 7.1 %collective-permute-start.7 = (f32[32,1280]{1,0:T(8,128)S(1)}, f32[32,1280]{1,0:T(8,128)S(1)}, u32[]{:S(2)}, u32[]{:S(2)}) collective-permute-start(f32[32,1280]{1,0:T(8,128)S(1)} %constant_dynamic-slice_fusion.6), channel_id=1, source_target_pairs={{0,1},{1,0},{2,3},{3,2},{4,5},{5,4},{6,7},{7,6},{8,9},{9,8},{10,11... | collective-permute-start | bytes 491528 | tf_op jit(solution)/shard_map/ppermute | solution.py:191
  72.9 8.3 %collective-permute-start.8 = (f32[32,1280]{1,0:T(8,128)S(1)}, f32[32,1280]{1,0:T(8,128)S(1)}, u32[]{:S(2)}, u32[]{:S(2)}) collective-permute-start(f32[32,1280]{1,0:T(8,128)S(1)} %constant_dynamic-slice_fusion.5), channel_id=1, source_target_pairs={{0,1},{1,0},{2,3},{3,2},{4,5},{5,4},{6,7},{7,6},{8,9},{9,8},{10,11... | collective-permute-start | bytes 491528 | tf_op jit(solution)/shard_map/ppermute | solution.py:191
  74.0 10.7 %collective-permute-start.9 = (f32[32,1280]{1,0:T(8,128)S(1)}, f32[32,1280]{1,0:T(8,128)S(1)}, u32[]{:S(2)}, u32[]{:S(2)}) collective-permute-start(f32[32,1280]{1,0:T(8,128)S(1)} %constant_dynamic-slice_fusion.4), channel_id=1, source_target_pairs={{0,1},{1,0},{2,3},{3,2},{4,5},{5,4},{6,7},{7,6},{8,9},{9,8},{10,11... | collective-permute-start | bytes 491528 | tf_op jit(solution)/shard_map/ppermute | solution.py:191
  75.0 13.0 %collective-permute-start.13 = (f32[32,1280]{1,0:T(8,128)S(1)}, f32[32,1280]{1,0:T(8,128)S(1)}, u32[]{:S(2)}, u32[]{:S(2)}) collective-permute-start(f32[32,1280]{1,0:T(8,128)S(1)} %constant_dynamic-slice_fusion.3), channel_id=1, source_target_pairs={{0,1},{1,0},{2,3},{3,2},{4,5},{5,4},{6,7},{7,6},{8,9},{9,8},{10,11... | collective-permute-start | bytes 491528 | tf_op jit(solution)/shard_map/ppermute | solution.py:191
  76.1 13.6 %collective-permute-start.14 = (f32[32,1280]{1,0:T(8,128)S(1)}, f32[32,1280]{1,0:T(8,128)S(1)}, u32[]{:S(2)}, u32[]{:S(2)}) collective-permute-start(f32[32,1280]{1,0:T(8,128)S(1)} %constant_dynamic-slice_fusion.2), channel_id=1, source_target_pairs={{0,1},{1,0},{2,3},{3,2},{4,5},{5,4},{6,7},{7,6},{8,9},{9,8},{10,11... | collective-permute-start | bytes 491528 | tf_op jit(solution)/shard_map/ppermute | solution.py:191
  77.7 13.8 %collective-permute-start.15 = (f32[32,1280]{1,0:T(8,128)S(1)}, f32[32,1280]{1,0:T(8,128)S(1)}, u32[]{:S(2)}, u32[]{:S(2)}) collective-permute-start(f32[32,1280]{1,0:T(8,128)S(1)} %constant_dynamic-slice_fusion.1), channel_id=1, source_target_pairs={{0,1},{1,0},{2,3},{3,2},{4,5},{5,4},{6,7},{7,6},{8,9},{9,8},{10,11... | collective-permute-start | bytes 491528 | tf_op jit(solution)/shard_map/ppermute | solution.py:191
  81.2 12.1 %collective-permute-start.16 = (f32[32,1280]{1,0:T(8,128)S(1)}, f32[32,1280]{1,0:T(8,128)S(1)}, u32[]{:S(2)}, u32[]{:S(2)}) collective-permute-start(f32[32,1280]{1,0:T(8,128)S(1)} %constant_dynamic-slice_fusion), channel_id=1, source_target_pairs={{0,1},{1,0},{2,3},{3,2},{4,5},{5,4},{6,7},{7,6},{8,9},{9,8},{10,11... | collective-permute-start | bytes 491528 | tf_op jit(solution)/shard_map/ppermute | solution.py:191
  85.3 10.2 %collective-permute-start.17 = (bf16[128,1280]{1,0:T(8,128)(2,1)S(1)}, bf16[128,1280]{1,0:T(8,128)(2,1)S(1)}, u32[]{:S(2)}, u32[]{:S(2)}) collective-permute-start(bf16[128,1280]{1,0:T(8,128)(2,1)S(1)} %shard_map.77.rest_0_), channel_id=1, source_target_pairs={{0,2},{2,4},{4,6},{6,0},{1,3},{3,5},{5,7},{7,1},{8,10},{10,12},{12... | collective-permute-start | bytes 983048 | tf_op jit(solution)/shard_map/ppermute | solution.py:186
  93.9 12.4 %collective-permute-start.18 = (bf16[128,1280]{1,0:T(8,128)(2,1)S(1)}, bf16[128,1280]{1,0:T(8,128)(2,1)S(1)}, u32[]{:S(2)}, u32[]{:S(2)}) collective-permute-start(bf16[128,1280]{1,0:T(8,128)(2,1)S(1)} %shard_map.78.rest_0_), channel_id=1, source_target_pairs={{0,2},{2,4},{4,6},{6,0},{1,3},{3,5},{5,7},{7,1},{8,10},{10,12},{12... | collective-permute-start | bytes 983048 | tf_op jit(solution)/shard_map/ppermute | solution.py:186
  95.5 17.8 %collective-permute-start.19 = (bf16[128,1280]{1,0:T(8,128)(2,1)S(1)}, bf16[128,1280]{1,0:T(8,128)(2,1)S(1)}, u32[]{:S(2)}, u32[]{:S(2)}) collective-permute-start(bf16[128,1280]{1,0:T(8,128)(2,1)S(1)} %collective-permute-done.17.rest_1_), channel_id=1, source_target_pairs={{0,2},{2,4},{4,6},{6,0},{1,3},{3,5},{5,7},{7,1},{8,10},{10,12},{12... | collective-permute-start | bytes 983048 | tf_op jit(solution)/shard_map/ppermute | solution.py:186
  106.4 14.0 %collective-permute-start.20 = (bf16[128,1280]{1,0:T(8,128)(2,1)S(1)}, bf16[128,1280]{1,0:T(8,128)(2,1)S(1)}, u32[]{:S(2)}, u32[]{:S(2)}) collective-permute-start(bf16[128,1280]{1,0:T(8,128)(2,1)S(1)} %collective-permute-done.18.rest_1_), channel_id=1, source_target_pairs={{0,2},{2,4},{4,6},{6,0},{1,3},{3,5},{5,7},{7,1},{8,10},{10,12},{12... | collective-permute-start | bytes 983048 | tf_op jit(solution)/shard_map/ppermute | solution.py:186
  106.5 15.4 %collective-permute-start.23 = (bf16[128,1280]{1,0:T(8,128)(2,1)S(1)}, bf16[128,1280]{1,0:T(8,128)(2,1)S(1)}, u32[]{:S(2)}, u32[]{:S(2)}) collective-permute-start(bf16[128,1280]{1,0:T(8,128)(2,1)S(1)} %shard_map.77.rest_0_), channel_id=1, source_target_pairs={{0,1},{1,0},{2,3},{3,2},{4,5},{5,4},{6,7},{7,6},{8,9},{9,8},{10,11... | collective-permute-start | bytes 983048 | tf_op jit(solution)/shard_map/ppermute | solution.py:191
  113.4 12.5 %collective-permute-start.21 = (bf16[128,1280]{1,0:T(8,128)(2,1)S(1)}, bf16[128,1280]{1,0:T(8,128)(2,1)S(1)}, u32[]{:S(2)}, u32[]{:S(2)}) collective-permute-start(bf16[128,1280]{1,0:T(8,128)(2,1)S(1)} %collective-permute-done.19.rest_2_), channel_id=1, source_target_pairs={{0,2},{2,4},{4,6},{6,0},{1,3},{3,5},{5,7},{7,1},{8,10},{10,12},{12... | collective-permute-start | bytes 983048 | tf_op jit(solution)/shard_map/ppermute | solution.py:186
  113.6 13.3 %collective-permute-start.24 = (bf16[128,1280]{1,0:T(8,128)(2,1)S(1)}, bf16[128,1280]{1,0:T(8,128)(2,1)S(1)}, u32[]{:S(2)}, u32[]{:S(2)}) collective-permute-start(bf16[128,1280]{1,0:T(8,128)(2,1)S(1)} %collective-permute-done.17.rest_1_), channel_id=1, source_target_pairs={{0,1},{1,0},{2,3},{3,2},{4,5},{5,4},{6,7},{7,6},{8,9},{9,8},{10,11... | collective-permute-start | bytes 983048 | tf_op jit(solution)/shard_map/ppermute | solution.py:191
  120.4 10.9 %collective-permute-start.29 = (bf16[128,1280]{1,0:T(8,128)(2,1)S(1)}, bf16[128,1280]{1,0:T(8,128)(2,1)S(1)}, u32[]{:S(2)}, u32[]{:S(2)}) collective-permute-start(bf16[128,1280]{1,0:T(8,128)(2,1)S(1)} %collective-permute-done.20.rest_2_), channel_id=1, source_target_pairs={{0,1},{1,0},{2,3},{3,2},{4,5},{5,4},{6,7},{7,6},{8,9},{9,8},{10,11... | collective-permute-start | bytes 983048 | tf_op jit(solution)/shard_map/ppermute | solution.py:191
  121.8 10.9 %collective-permute-start.22 = (bf16[128,1280]{1,0:T(8,128)(2,1)S(1)}, bf16[128,1280]{1,0:T(8,128)(2,1)S(1)}, u32[]{:S(2)}, u32[]{:S(2)}) collective-permute-start(bf16[128,1280]{1,0:T(8,128)(2,1)S(1)} %collective-permute-done.20.rest_2_), channel_id=1, source_target_pairs={{0,2},{2,4},{4,6},{6,0},{1,3},{3,5},{5,7},{7,1},{8,10},{10,12},{12... | collective-permute-start | bytes 983048 | tf_op jit(solution)/shard_map/ppermute | solution.py:186
  121.9 16.4 %collective-permute-start.25 = (bf16[128,1280]{1,0:T(8,128)(2,1)S(1)}, bf16[128,1280]{1,0:T(8,128)(2,1)S(1)}, u32[]{:S(2)}, u32[]{:S(2)}) collective-permute-start(bf16[128,1280]{1,0:T(8,128)(2,1)S(1)} %collective-permute-done.19.rest_2_), channel_id=1, source_target_pairs={{0,1},{1,0},{2,3},{3,2},{4,5},{5,4},{6,7},{7,6},{8,9},{9,8},{10,11... | collective-permute-start | bytes 983048 | tf_op jit(solution)/shard_map/ppermute | solution.py:191
  125.9 19.3 %collective-permute-start.26 = (bf16[128,1280]{1,0:T(8,128)(2,1)S(1)}, bf16[128,1280]{1,0:T(8,128)(2,1)S(1)}, u32[]{:S(2)}, u32[]{:S(2)}) collective-permute-start(bf16[128,1280]{1,0:T(8,128)(2,1)S(1)} %collective-permute-done.21.rest_3_), channel_id=1, source_target_pairs={{0,1},{1,0},{2,3},{3,2},{4,5},{5,4},{6,7},{7,6},{8,9},{9,8},{10,11... | collective-permute-start | bytes 983048 | tf_op jit(solution)/shard_map/ppermute | solution.py:191
  126.9 27.4 %collective-permute-start.27 = (bf16[128,1280]{1,0:T(8,128)(2,1)S(1)}, bf16[128,1280]{1,0:T(8,128)(2,1)S(1)}, u32[]{:S(2)}, u32[]{:S(2)}) collective-permute-start(bf16[128,1280]{1,0:T(8,128)(2,1)S(1)} %shard_map.78.rest_0_), channel_id=1, source_target_pairs={{0,1},{1,0},{2,3},{3,2},{4,5},{5,4},{6,7},{7,6},{8,9},{9,8},{10,11... | collective-permute-start | bytes 983048 | tf_op jit(solution)/shard_map/ppermute | solution.py:191
  131.3 23.1 %collective-permute-start.28 = (bf16[128,1280]{1,0:T(8,128)(2,1)S(1)}, bf16[128,1280]{1,0:T(8,128)(2,1)S(1)}, u32[]{:S(2)}, u32[]{:S(2)}) collective-permute-start(bf16[128,1280]{1,0:T(8,128)(2,1)S(1)} %collective-permute-done.18.rest_1_), channel_id=1, source_target_pairs={{0,1},{1,0},{2,3},{3,2},{4,5},{5,4},{6,7},{7,6},{8,9},{9,8},{10,11... | collective-permute-start | bytes 983048 | tf_op jit(solution)/shard_map/ppermute | solution.py:191
  132.6 21.8 %collective-permute-start.30 = (bf16[128,1280]{1,0:T(8,128)(2,1)S(1)}, bf16[128,1280]{1,0:T(8,128)(2,1)S(1)}, u32[]{:S(2)}, u32[]{:S(2)}) collective-permute-start(bf16[128,1280]{1,0:T(8,128)(2,1)S(1)} %collective-permute-done.29.rest_6_), channel_id=1, source_target_pairs={{0,2},{2,4},{4,6},{6,0},{1,3},{3,5},{5,7},{7,1},{8,10},{10,12},{12... | collective-permute-start | bytes 983048 | tf_op jit(solution)/shard_map/ppermute | solution.py:186
  164.2 11.2 %all-to-all-start = ((f32[8,1,192]{2,1,0:T(1,128)}), f32[8,1,192]{2,1,0:T(1,128)S(1)}, u32[]{:S(2)}, u32[]{:S(2)}) async-start(f32[8,1,192]{2,1,0:T(1,128)} %shard_map.80), calls=%async_computation | async-start | bytes 16384 | tf_op jit(solution)/shard_map/all_to_all | solution.py:252
  (6 other events, 165.1 us)
